TPU v7x, 32 devices: a whole 2x2x4 slice. The times are simulated.
32 devices in a mesh: box: 2 (over x), dir: 16 (over z, y, core).
Axes of the slice: x: 2, y: 2, z: 4, core: 2. Of those that a mesh axis runs over, the one named last changes fastest.
Arguments:
- leaf_patterns: bfloat16 [512, 2, 8, 1024], P(('box', 'dir')), may hold values from -6 to 6
- octant: int32 [512], P(('box', 'dir')), may hold values from 0 to 7, as said below
- interp: bfloat16 [1024, 4096], replicated, may hold values from -0.1875 to 0.1875
- shift_angle: float32 [8, 4096], replicated, may hold values from -3.140625 to 3.140625
- partners: int32 [64, 27], P('box'), may hold values from 0 to 63, as said below
- types: int32 [64, 27], P('box'), may hold values from 0 to 342, as said below
- translators: float32 [343, 2, 4096], P(None, None, 'dir'), may hold values from -1 to 1
Outputs:
- leaf_incoming: bfloat16 [512, 2, 8, 1024], P(('box', 'dir'))
Inputs may be any that keep to these rules, and one draw needn't show every extreme that they name: The leaf boxes 8 p to 8 p + 7 are the children of parent box p; octant gives each child its position in the parent, each of 0 to 7 once among the 8 children. Parent boxes form a grid indexed in Morton order (bit j of the index is a bit of coordinate j % 3). The 27 partners of a box are distinct boxes within three boxes of it along every dimension, and none is the box itself or one of its 26 neighbours. types[p, k] = 49 (dx + 3) + 7 (dy + 3) + (dz + 3), where (dx, dy, dz) is the grid offset from box p to partners[p, k].
All inputs are finite; a program needn't handle non-finite values.
Results may differ from a plain program's by a relative error of at most 0.0064.
Values may be sent and summed in bfloat16 or wider, within the bound.
No kernel may reach another device: no remote copies, remote signals or barrier semaphores. Data moves between devices by JAX's collectives and lax.ppermute only.
A program may use at most 64 MiB of HBM per device.

v0:
```python
import jax
import jax.numpy as jnp
from jax import lax
from jax.sharding import PartitionSpec as P


def local(leaf_patterns, octant, interp, shift_angle, partners, types, translators):
    boxes, pairs, excite, low = leaf_patterns.shape
    high = interp.shape[1]
    groups = lax.axis_size("dir")
    width = high // groups
    parents = boxes // 8
    columns = 2 * excite * width
    cosines = jnp.cos(shift_angle)
    sines = jnp.sin(shift_angle)
    select = (octant[:, None] == jnp.arange(8, dtype=jnp.int32)[None, :]).astype(jnp.float32)
    child_cos = jnp.dot(select, cosines, precision=lax.Precision.HIGHEST)[:, None, :]
    child_sin = jnp.dot(select, sines, precision=lax.Precision.HIGHEST)[:, None, :]
    up = jnp.dot(leaf_patterns.reshape(-1, low), interp, preferred_element_type=jnp.float32)
    up = up.reshape(boxes, 2, excite, high)
    real = up[:, 0] * child_cos - up[:, 1] * child_sin
    imag = up[:, 0] * child_sin + up[:, 1] * child_cos
    aggregated = (
        jnp.stack([real, imag], 1)
        .reshape(parents, 8, 2, excite, high)
        .sum(axis=1)
        .astype(jnp.bfloat16)
    )
    outgoing = aggregated.reshape(parents, 2, excite, groups, width).transpose(0, 3, 1, 2, 4)
    outgoing = outgoing.reshape(parents, groups, columns)
    regrouped = lax.all_to_all(outgoing, "dir", split_axis=1, concat_axis=0, tiled=True).reshape(
        parents * groups, columns
    )
    every = lax.all_gather(regrouped, "box", axis=0, tiled=True)
    owned = partners.shape[0]
    linked = partners.shape[1]

    def translate(step, total):
        source = (
            jnp.take(every, partners[:, step], axis=0)
            .reshape(owned, 2, excite, width)
            .astype(jnp.float32)
        )
        factor = jnp.take(translators, types[:, step], axis=0)
        factor_re = factor[:, 0][:, None, :]
        factor_im = factor[:, 1][:, None, :]
        real_part = factor_re * source[:, 0] - factor_im * source[:, 1]
        imag_part = factor_re * source[:, 1] + factor_im * source[:, 0]
        return total + jnp.stack([real_part, imag_part], 1)

    zero = jnp.zeros((owned, 2, excite, width), jnp.float32)
    summed = lax.fori_loop(0, linked, translate, zero)
    incoming = summed.astype(jnp.bfloat16).reshape(groups, parents, 1, columns)
    returned = lax.all_to_all(incoming, "dir", split_axis=0, concat_axis=2, tiled=True)
    returned = returned.reshape(parents, groups, 2, excite, width).transpose(0, 2, 3, 1, 4)
    returned = returned.reshape(parents, 1, 2, excite, high).astype(jnp.float32)
    spread_cos = child_cos.reshape(parents, 8, 1, 1, high)
    spread_sin = child_sin.reshape(parents, 8, 1, 1, high)
    real = returned[:, :, 0] * spread_cos[:, :, 0] + returned[:, :, 1] * spread_sin[:, :, 0]
    imag = returned[:, :, 1] * spread_cos[:, :, 0] - returned[:, :, 0] * spread_sin[:, :, 0]
    shifted = jnp.stack([real, imag], 2).astype(jnp.bfloat16).reshape(-1, high)
    down = lax.dot_general(
        shifted, interp, (((1,), (1,)), ((), ())), preferred_element_type=jnp.float32
    )
    scale = low / high
    return (down * scale).astype(jnp.bfloat16).reshape(boxes, 2, excite, low)


def solution(mesh):
    placed = (
        P(("box", "dir"), None, None, None),
        P(("box", "dir")),
        P(),
        P(),
        P("box", None),
        P("box", None),
        P(None, None, "dir"),
    )
    return jax.shard_map(
        local,
        mesh=mesh,
        in_specs=placed,
        out_specs=P(("box", "dir"), None, None, None),
        check_vma=False,
    )
```

profile of v0, /device:TPU:0, one launch (start us, length us, event | category | flops | bytes accessed | tf_op | source)
XLA Modules:
  0.0 143.4 jit_solution(12778641623120094135)
XLA Ops:
  0.0 1.6 %fusion.3 = f32[16,4096]{1,0:T(8,128)S(1)} fusion(f32[8,4096]{1,0:T(8,128)} %param.12, s32[16]{0:T(128)} %param.10), kind=kOutput, calls=%fused_computation.28 | convolution fusion | flops 6291584 | bytes 393280 | tf_op jit(solution)/shard_map/dot_general | solution.py:18
  1.6 1.6 %fusion.5 = f32[16,4096]{1,0:T(8,128)S(1)} fusion(f32[8,4096]{1,0:T(8,128)} %param.12, s32[16]{0:T(128)} %param.10), kind=kOutput, calls=%fused_computation.30 | convolution fusion | flops 6291584 | bytes 393280 | tf_op jit(solution)/shard_map/dot_general | solution.py:17
  3.2 5.7 %fusion = f32[16,2,8,4096]{3,2,1,0:T(8,128)S(1)} fusion(bf16[16,2,8,1024]{3,2,1,0:T(8,128)(2,1)S(1)} %copy-done, bf16[1024,4096]{1,0:T(8,128)(2,1)} %param.11), kind=kOutput, calls=%fused_computation.15 | convolution fusion | flops 2147483648 | bytes 13107200 | tf_op jit(solution)/shard_map/dot_general | solution.py:19
  9.0 0.7 multiply_subtract_fusion.1
  10.0 0.8 reshape.124
  10.7 7.4 %all-to-all-start = ((bf16[2,16,4096]{2,0,1:T(2,128)(2,1)}), bf16[2,16,4096]{2,0,1:T(2,128)(2,1)S(1)}, u32[]{:S(2)}, u32[]{:S(2)}) async-start(bf16[2,16,4096]{2,0,1:T(2,128)(2,1)} %reshape.124), calls=%async_computation | async-start | bytes 524288 | tf_op jit(solution)/shard_map/all_to_all | solution.py:31
  18.4 9.8 %all-to-all-done = bf16[2,16,4096]{2,0,1:T(2,128)(2,1)S(1)} async-done(((bf16[2,16,4096]{2,0,1:T(2,128)(2,1)}), bf16[2,16,4096]{2,0,1:T(2,128)(2,1)S(1)}, u32[]{:S(2)}, u32[]{:S(2)}) %all-to-all-start) | async-done | bytes 262176 | tf_op jit(solution)/shard_map/all_to_all | solution.py:31
  28.3 8.8 %all_gather.3 = bf16[64,4096]{1,0:T(8,128)(2,1)S(1)} all-gather(bf16[32,4096]{1,0:T(8,128)(2,1)S(1)} %reshape.94), channel_id=1, replica_groups=mesh['box'=2,'dir'=16] {'box'}, dimensions={0}, use_global_device_ids=true | all-gather | bytes 786432 | tf_op jit(solution)/shard_map/all_gather | solution.py:34
  37.1 84.7 %while.14 = (s32[]{:T(128)}, f32[32,2,8,256]{3,2,1,0:T(8,128)S(1)}, s32[32,27]{0,1:T(8,128)S(1)}, f32[343,2,256]{2,1,0:T(2,128)}, s32[32,27]{0,1:T(8,128)S(1)}, ...) while((s32[]{:T(128)}, f32[32,2,8,256]{3,2,1,0:T(8,128)S(1)}, s32[32,27]{0,1:T(8,128)S(1)}, ...), condition=%wide.region_2.0_spmd.clone, body=%wide.region_1.2_spmd.clone.sunk | while | flops 1067395 | bytes 5055715 | solution.py:52
  37.1 1.7 %gather_fusion.1 = f32[32,2,256]{2,1,0:T(2,128)S(1)} fusion(f32[343,2,256]{2,1,0:T(2,128)} %get-tuple-element.266, s32[1024]{0:T(1024)S(1)} %pad_clamp_fusion.5), kind=kCustom, calls=%fused_computation.clone.clone.1 | custom fusion | bytes 131200 | tf_op jit(solution)/shard_map/while/body/eval_jaxpr/jit(_take)/gather | solution.py:44
  39.0 0.7 gather_fusion
  40.2 1.7 %gather_fusion.1 = f32[32,2,256]{2,1,0:T(2,128)S(1)} fusion(f32[343,2,256]{2,1,0:T(2,128)} %get-tuple-element.266, s32[1024]{0:T(1024)S(1)} %pad_clamp_fusion.5), kind=kCustom, calls=%fused_computation.clone.clone.1 | custom fusion | bytes 131200 | tf_op jit(solution)/shard_map/while/body/eval_jaxpr/jit(_take)/gather | solution.py:44
  42.2 0.7 gather_fusion
  43.4 1.7 %gather_fusion.1 = f32[32,2,256]{2,1,0:T(2,128)S(1)} fusion(f32[343,2,256]{2,1,0:T(2,128)} %get-tuple-element.266, s32[1024]{0:T(1024)S(1)} %pad_clamp_fusion.5), kind=kCustom, calls=%fused_computation.clone.clone.1 | custom fusion | bytes 131200 | tf_op jit(solution)/shard_map/while/body/eval_jaxpr/jit(_take)/gather | solution.py:44
  45.3 0.7 gather_fusion
  46.5 1.7 %gather_fusion.1 = f32[32,2,256]{2,1,0:T(2,128)S(1)} fusion(f32[343,2,256]{2,1,0:T(2,128)} %get-tuple-element.266, s32[1024]{0:T(1024)S(1)} %pad_clamp_fusion.5), kind=kCustom, calls=%fused_computation.clone.clone.1 | custom fusion | bytes 131200 | tf_op jit(solution)/shard_map/while/body/eval_jaxpr/jit(_take)/gather | solution.py:44
  48.5 0.7 gather_fusion
  49.6 1.7 %gather_fusion.1 = f32[32,2,256]{2,1,0:T(2,128)S(1)} fusion(f32[343,2,256]{2,1,0:T(2,128)} %get-tuple-element.266, s32[1024]{0:T(1024)S(1)} %pad_clamp_fusion.5), kind=kCustom, calls=%fused_computation.clone.clone.1 | custom fusion | bytes 131200 | tf_op jit(solution)/shard_map/while/body/eval_jaxpr/jit(_take)/gather | solution.py:44
  51.6 0.7 gather_fusion
  52.8 1.7 %gather_fusion.1 = f32[32,2,256]{2,1,0:T(2,128)S(1)} fusion(f32[343,2,256]{2,1,0:T(2,128)} %get-tuple-element.266, s32[1024]{0:T(1024)S(1)} %pad_clamp_fusion.5), kind=kCustom, calls=%fused_computation.clone.clone.1 | custom fusion | bytes 131200 | tf_op jit(solution)/shard_map/while/body/eval_jaxpr/jit(_take)/gather | solution.py:44
  54.7 0.7 gather_fusion
  55.9 1.7 %gather_fusion.1 = f32[32,2,256]{2,1,0:T(2,128)S(1)} fusion(f32[343,2,256]{2,1,0:T(2,128)} %get-tuple-element.266, s32[1024]{0:T(1024)S(1)} %pad_clamp_fusion.5), kind=kCustom, calls=%fused_computation.clone.clone.1 | custom fusion | bytes 131200 | tf_op jit(solution)/shard_map/while/body/eval_jaxpr/jit(_take)/gather | solution.py:44
  57.9 0.7 gather_fusion
  59.1 1.7 %gather_fusion.1 = f32[32,2,256]{2,1,0:T(2,128)S(1)} fusion(f32[343,2,256]{2,1,0:T(2,128)} %get-tuple-element.266, s32[1024]{0:T(1024)S(1)} %pad_clamp_fusion.5), kind=kCustom, calls=%fused_computation.clone.clone.1 | custom fusion | bytes 131200 | tf_op jit(solution)/shard_map/while/body/eval_jaxpr/jit(_take)/gather | solution.py:44
  61.0 0.7 gather_fusion
  62.2 1.7 %gather_fusion.1 = f32[32,2,256]{2,1,0:T(2,128)S(1)} fusion(f32[343,2,256]{2,1,0:T(2,128)} %get-tuple-element.266, s32[1024]{0:T(1024)S(1)} %pad_clamp_fusion.5), kind=kCustom, calls=%fused_computation.clone.clone.1 | custom fusion | bytes 131200 | tf_op jit(solution)/shard_map/while/body/eval_jaxpr/jit(_take)/gather | solution.py:44
  64.2 0.7 gather_fusion
  65.3 1.7 %gather_fusion.1 = f32[32,2,256]{2,1,0:T(2,128)S(1)} fusion(f32[343,2,256]{2,1,0:T(2,128)} %get-tuple-element.266, s32[1024]{0:T(1024)S(1)} %pad_clamp_fusion.5), kind=kCustom, calls=%fused_computation.clone.clone.1 | custom fusion | bytes 131200 | tf_op jit(solution)/shard_map/while/body/eval_jaxpr/jit(_take)/gather | solution.py:44
  67.3 0.7 gather_fusion
  68.5 1.7 %gather_fusion.1 = f32[32,2,256]{2,1,0:T(2,128)S(1)} fusion(f32[343,2,256]{2,1,0:T(2,128)} %get-tuple-element.266, s32[1024]{0:T(1024)S(1)} %pad_clamp_fusion.5), kind=kCustom, calls=%fused_computation.clone.clone.1 | custom fusion | bytes 131200 | tf_op jit(solution)/shard_map/while/body/eval_jaxpr/jit(_take)/gather | solution.py:44
  70.4 0.7 gather_fusion
  71.6 1.7 %gather_fusion.1 = f32[32,2,256]{2,1,0:T(2,128)S(1)} fusion(f32[343,2,256]{2,1,0:T(2,128)} %get-tuple-element.266, s32[1024]{0:T(1024)S(1)} %pad_clamp_fusion.5), kind=kCustom, calls=%fused_computation.clone.clone.1 | custom fusion | bytes 131200 | tf_op jit(solution)/shard_map/while/body/eval_jaxpr/jit(_take)/gather | solution.py:44
  73.6 0.7 gather_fusion
  74.8 1.7 %gather_fusion.1 = f32[32,2,256]{2,1,0:T(2,128)S(1)} fusion(f32[343,2,256]{2,1,0:T(2,128)} %get-tuple-element.266, s32[1024]{0:T(1024)S(1)} %pad_clamp_fusion.5), kind=kCustom, calls=%fused_computation.clone.clone.1 | custom fusion | bytes 131200 | tf_op jit(solution)/shard_map/while/body/eval_jaxpr/jit(_take)/gather | solution.py:44
  76.7 0.7 gather_fusion
  77.9 1.7 %gather_fusion.1 = f32[32,2,256]{2,1,0:T(2,128)S(1)} fusion(f32[343,2,256]{2,1,0:T(2,128)} %get-tuple-element.266, s32[1024]{0:T(1024)S(1)} %pad_clamp_fusion.5), kind=kCustom, calls=%fused_computation.clone.clone.1 | custom fusion | bytes 131200 | tf_op jit(solution)/shard_map/while/body/eval_jaxpr/jit(_take)/gather | solution.py:44
  79.8 0.7 gather_fusion
  81.0 1.7 %gather_fusion.1 = f32[32,2,256]{2,1,0:T(2,128)S(1)} fusion(f32[343,2,256]{2,1,0:T(2,128)} %get-tuple-element.266, s32[1024]{0:T(1024)S(1)} %pad_clamp_fusion.5), kind=kCustom, calls=%fused_computation.clone.clone.1 | custom fusion | bytes 131200 | tf_op jit(solution)/shard_map/while/body/eval_jaxpr/jit(_take)/gather | solution.py:44
  83.0 0.7 gather_fusion
  84.2 1.7 %gather_fusion.1 = f32[32,2,256]{2,1,0:T(2,128)S(1)} fusion(f32[343,2,256]{2,1,0:T(2,128)} %get-tuple-element.266, s32[1024]{0:T(1024)S(1)} %pad_clamp_fusion.5), kind=kCustom, calls=%fused_computation.clone.clone.1 | custom fusion | bytes 131200 | tf_op jit(solution)/shard_map/while/body/eval_jaxpr/jit(_take)/gather | solution.py:44
  86.1 0.7 gather_fusion
  87.3 1.7 %gather_fusion.1 = f32[32,2,256]{2,1,0:T(2,128)S(1)} fusion(f32[343,2,256]{2,1,0:T(2,128)} %get-tuple-element.266, s32[1024]{0:T(1024)S(1)} %pad_clamp_fusion.5), kind=kCustom, calls=%fused_computation.clone.clone.1 | custom fusion | bytes 131200 | tf_op jit(solution)/shard_map/while/body/eval_jaxpr/jit(_take)/gather | solution.py:44
  89.3 0.7 gather_fusion
  90.4 1.7 %gather_fusion.1 = f32[32,2,256]{2,1,0:T(2,128)S(1)} fusion(f32[343,2,256]{2,1,0:T(2,128)} %get-tuple-element.266, s32[1024]{0:T(1024)S(1)} %pad_clamp_fusion.5), kind=kCustom, calls=%fused_computation.clone.clone.1 | custom fusion | bytes 131200 | tf_op jit(solution)/shard_map/while/body/eval_jaxpr/jit(_take)/gather | solution.py:44
  92.4 0.7 gather_fusion
  93.6 1.7 %gather_fusion.1 = f32[32,2,256]{2,1,0:T(2,128)S(1)} fusion(f32[343,2,256]{2,1,0:T(2,128)} %get-tuple-element.266, s32[1024]{0:T(1024)S(1)} %pad_clamp_fusion.5), kind=kCustom, calls=%fused_computation.clone.clone.1 | custom fusion | bytes 131200 | tf_op jit(solution)/shard_map/while/body/eval_jaxpr/jit(_take)/gather | solution.py:44
  95.5 0.7 gather_fusion
  96.7 1.7 %gather_fusion.1 = f32[32,2,256]{2,1,0:T(2,128)S(1)} fusion(f32[343,2,256]{2,1,0:T(2,128)} %get-tuple-element.266, s32[1024]{0:T(1024)S(1)} %pad_clamp_fusion.5), kind=kCustom, calls=%fused_computation.clone.clone.1 | custom fusion | bytes 131200 | tf_op jit(solution)/shard_map/while/body/eval_jaxpr/jit(_take)/gather | solution.py:44
  98.7 0.7 gather_fusion
  99.9 1.7 %gather_fusion.1 = f32[32,2,256]{2,1,0:T(2,128)S(1)} fusion(f32[343,2,256]{2,1,0:T(2,128)} %get-tuple-element.266, s32[1024]{0:T(1024)S(1)} %pad_clamp_fusion.5), kind=kCustom, calls=%fused_computation.clone.clone.1 | custom fusion | bytes 131200 | tf_op jit(solution)/shard_map/while/body/eval_jaxpr/jit(_take)/gather | solution.py:44
  101.8 0.7 gather_fusion
  103.0 1.7 %gather_fusion.1 = f32[32,2,256]{2,1,0:T(2,128)S(1)} fusion(f32[343,2,256]{2,1,0:T(2,128)} %get-tuple-element.266, s32[1024]{0:T(1024)S(1)} %pad_clamp_fusion.5), kind=kCustom, calls=%fused_computation.clone.clone.1 | custom fusion | bytes 131200 | tf_op jit(solution)/shard_map/while/body/eval_jaxpr/jit(_take)/gather | solution.py:44
  104.9 0.7 gather_fusion
  106.1 1.7 %gather_fusion.1 = f32[32,2,256]{2,1,0:T(2,128)S(1)} fusion(f32[343,2,256]{2,1,0:T(2,128)} %get-tuple-element.266, s32[1024]{0:T(1024)S(1)} %pad_clamp_fusion.5), kind=kCustom, calls=%fused_computation.clone.clone.1 | custom fusion | bytes 131200 | tf_op jit(solution)/shard_map/while/body/eval_jaxpr/jit(_take)/gather | solution.py:44
  108.1 0.7 gather_fusion
  109.3 1.7 %gather_fusion.1 = f32[32,2,256]{2,1,0:T(2,128)S(1)} fusion(f32[343,2,256]{2,1,0:T(2,128)} %get-tuple-element.266, s32[1024]{0:T(1024)S(1)} %pad_clamp_fusion.5), kind=kCustom, calls=%fused_computation.clone.clone.1 | custom fusion | bytes 131200 | tf_op jit(solution)/shard_map/while/body/eval_jaxpr/jit(_take)/gather | solution.py:44
  111.2 0.7 gather_fusion
  112.4 1.7 %gather_fusion.1 = f32[32,2,256]{2,1,0:T(2,128)S(1)} fusion(f32[343,2,256]{2,1,0:T(2,128)} %get-tuple-element.266, s32[1024]{0:T(1024)S(1)} %pad_clamp_fusion.5), kind=kCustom, calls=%fused_computation.clone.clone.1 | custom fusion | bytes 131200 | tf_op jit(solution)/shard_map/while/body/eval_jaxpr/jit(_take)/gather | solution.py:44
  114.4 0.7 gather_fusion
  115.5 1.7 %gather_fusion.1 = f32[32,2,256]{2,1,0:T(2,128)S(1)} fusion(f32[343,2,256]{2,1,0:T(2,128)} %get-tuple-element.266, s32[1024]{0:T(1024)S(1)} %pad_clamp_fusion.5), kind=kCustom, calls=%fused_computation.clone.clone.1 | custom fusion | bytes 131200 | tf_op jit(solution)/shard_map/while/body/eval_jaxpr/jit(_take)/gather | solution.py:44
  117.5 0.7 gather_fusion
  118.7 1.7 %gather_fusion.1 = f32[32,2,256]{2,1,0:T(2,128)S(1)} fusion(f32[343,2,256]{2,1,0:T(2,128)} %get-tuple-element.266, s32[1024]{0:T(1024)S(1)} %pad_clamp_fusion.5), kind=kCustom, calls=%fused_computation.clone.clone.1 | custom fusion | bytes 131200 | tf_op jit(solution)/shard_map/while/body/eval_jaxpr/jit(_take)/gather | solution.py:44
  121.9 13.1 %all_to_all.27 = bf16[16,2,1,4096]{3,1,2,0:T(2,128)(2,1)S(1)} all-to-all(bf16[16,2,1,4096]{3,1,2,0:T(2,128)(2,1)S(1)} %reshape.95), channel_id=1, replica_groups=mesh['box'=2,'dir'=16] {'dir'}, dimensions={0} | all-to-all | bytes 524288 | tf_op jit(solution)/shard_map/all_to_all | solution.py:54
  136.8 6.5 %fusion.2 = bf16[256,1024]{1,0:T(8,128)(2,1)} fusion(bf16[256,4096]{1,0:T(8,128)(2,1)S(1)} %bitcast.89, bf16[1024,4096]{1,0:T(8,128)(2,1)} %param.11), kind=kOutput, calls=%fused_computation.24 | convolution fusion | flops 2148007936 | bytes 11010048 | tf_op jit(solution)/shard_map/dot_general | solution.py:62
  (319 shorter events, 18.7 us)
Async XLA Ops:
  0.0 3.2 %copy-start = (bf16[16,2,8,1024]{3,2,1,0:T(8,128)(2,1)S(1)}, bf16[16,2,8,1024]{3,2,1,0:T(8,128)(2,1)}, u32[]{:S(2)}) copy-start(bf16[16,2,8,1024]{3,2,1,0:T(8,128)(2,1)} %param.9) | copy-start | bytes 1572868
  9.7 8.5 %copy-start.1 = (s32[32,27]{1,0:T(8,128)S(1)}, s32[32,27]{1,0:T(8,128)}, u32[]{:S(2)}) copy-start(s32[32,27]{1,0:T(8,128)} %param.14) | copy-start | bytes 10372
  9.7 8.6 %copy-start.2 = (s32[32,27]{1,0:T(8,128)S(1)}, s32[32,27]{1,0:T(8,128)}, u32[]{:S(2)}) copy-start(s32[32,27]{1,0:T(8,128)} %param.13) | copy-start | bytes 10372
  10.7 17.4 %all-to-all-start = ((bf16[2,16,4096]{2,0,1:T(2,128)(2,1)}), bf16[2,16,4096]{2,0,1:T(2,128)(2,1)S(1)}, u32[]{:S(2)}, u32[]{:S(2)}) async-start(bf16[2,16,4096]{2,0,1:T(2,128)(2,1)} %reshape.124), calls=%async_computation | async-start | bytes 524288 | tf_op jit(solution)/shard_map/all_to_all | solution.py:31
where the time goes:
time: 145 us; the launch traced here: 143 us
  local copies, waits for them, and re-layouts  71 us (49%)
  blocking collectives  21.8 us (15%)
  matrix products  15.5 us (11%)
  other arithmetic  14.5 us (10%)
  waiting for transfers between devices  9.83 us (7%)
  starting transfers between devices  7.41 us (5%)
  loops' own time  3.13 us (2%)
    gather x27, local copies, waits for them, and re-layouts, translate(): factor = jnp.take(translators, types[:, step], axis=0)  46.9 us
    gather x27, local copies, waits for them, and re-layouts, translate(): jnp.take(every, partners[:, step], axis=0).reshape(owned, 2, excite, width)  19.1 us
    all_to_all x1, blocking collectives, local(): lax.all_to_all(incoming, 'dir', split_axis=0, concat_axis=2, tiled=True)  13.1 us
    all_to_all x1, waiting for transfers between devices, local(): lax.all_to_all(outgoing, 'dir', split_axis=1, concat_axis=0, tiled=True)  9.83 us
    all_gather x1, blocking collectives, local(): every = lax.all_gather(regrouped, 'box', axis=0, tiled=True)  8.79 us
    all_to_all x1, starting transfers between devices, local(): lax.all_to_all(outgoing, 'dir', split_axis=1, concat_axis=0, tiled=True)  7.41 us
    dot_general x1, matrix products, local(): lax.dot_general(shifted, interp, (((1,), (1,)), ((), ())), preferred_elem...  6.54 us
    dot_general x1, matrix products, local(): jnp.dot(leaf_patterns.reshape(-1, low), interp, preferred_element_type=jn...  5.73 us
  transfers between devices with their start and end apart: 1, of which 1 were waited for; matrix products, arithmetic and copies ran while one was open for 0% of the time, Pallas kernels for 0%

commit v1 on v0

v1 whole, which is shorter than its diff:
```python
import functools

import jax
import jax.numpy as jnp
from jax import lax
from jax.experimental import pallas as pl
from jax.experimental.pallas import tpu as pltpu
from jax.sharding import PartitionSpec as P

LANES = 128
EXCITE = 8
PAIR = 2 * EXCITE
MIB = 1 << 20
AHEAD = 2


def sincos(x):
    turns = jnp.floor(x * 0.6366197723675814 + 0.5)
    r = x - turns * 1.5703125
    r = r - turns * 4.837512969970703e-4
    r = r - turns * 7.549789948768648e-8
    z = r * r
    s = ((-1.9515295891e-4 * z + 8.3321608736e-3) * z - 1.6666654611e-1) * z * r + r
    c = ((2.443315711809948e-5 * z - 1.388731625493765e-3) * z + 4.166664568298827e-2) * z * z
    c = c - 0.5 * z + 1.0
    quadrant = turns.astype(jnp.int32)
    odd = (quadrant & 1) == 1
    sine = jnp.where(odd, c, s)
    cosine = jnp.where(odd, s, c)
    sine = jnp.where((quadrant & 2) == 2, -sine, sine)
    cosine = jnp.where(((quadrant + 1) & 2) == 2, -cosine, cosine)
    return cosine, sine


def phases(angle, cosines, sines):
    def block(b, carry):
        lanes = pl.ds(pl.multiple_of(b * LANES, LANES), LANES)
        cosines[b], sines[b] = sincos(angle[:, lanes])
        return carry

    lax.fori_loop(0, cosines.shape[0], block, 0, unroll=4)


def chunk_of(i, tile):
    return pl.ds(pl.multiple_of(i * tile, tile), tile)


def column_copy(far, near, arrived, tile, i):
    columns = chunk_of(i, tile)
    return pltpu.make_async_copy(far.at[:, columns], near.at[:, columns], arrived.at[i])


def lift_kernel(
    place, tile, octant_far, leaf_far, interp_far, angle_far, out_far,
    octant, leaf, interp, angle, cosines, sines, up_even, up_odd, out, arrived, ready, sent,
):
    low, high = interp.shape
    count = high // tile
    boxes = leaf.shape[0] // PAIR
    angle_copy = pltpu.make_async_copy(angle_far, angle, ready.at[0])
    leaf_copy = pltpu.make_async_copy(leaf_far, leaf, ready.at[1])
    octant_copy = pltpu.make_async_copy(octant_far, octant, ready.at[2])
    angle_copy.start()
    octant_copy.start()
    leaf_copy.start()
    ahead = min(AHEAD, count)
    for i in range(ahead):
        column_copy(interp_far, interp, arrived, tile, i).start()
    angle_copy.wait()
    phases(angle, cosines, sines)
    octant_copy.wait()
    leaf_copy.wait()

    def send(i, first, last):
        for part in range(tile // LANES):
            block = place(i * (tile // LANES) + part)
            copy = pltpu.make_async_copy(out.at[block], out_far.at[block], sent.at[block])
            copy.start() if first else None
            copy.wait() if last else None

    def rise(i, up):
        column_copy(interp_far, interp, arrived, tile, i).wait()

        @pl.when(i + ahead < count)
        def _():
            column_copy(interp_far, interp, arrived, tile, i + ahead).start()

        up[...] = jnp.dot(
            leaf[...], interp[:, chunk_of(i, tile)], preferred_element_type=jnp.float32
        )

    def combine(i, up):
        for lane in range(0, tile, LANES):
            block = i * (tile // LANES) + lane // LANES
            for parent in range(boxes // 8):
                real = imag = None
                for child in range(8 * parent, 8 * parent + 8):
                    which = octant[child]
                    cos = cosines[block, pl.ds(which, 1), :]
                    sin = sines[block, pl.ds(which, 1), :]
                    row = PAIR * child
                    up_re = up[row : row + EXCITE, lane : lane + LANES]
                    up_im = up[row + EXCITE : row + PAIR, lane : lane + LANES]
                    re = up_re * cos - up_im * sin
                    im = up_re * sin + up_im * cos
                    real = re if real is None else real + re
                    imag = im if imag is None else imag + im
                both = jnp.concatenate([real, imag], 0).astype(jnp.bfloat16)
                out[place(block), PAIR * parent : PAIR * (parent + 1), :] = both

    def two(j, carry):
        @pl.when(j > 0)
        def _():
            send(2 * j - 2, True, False)

        rise(2 * j, up_even)
        combine(jnp.maximum(2 * j - 1, 0), up_odd)
        rise(2 * j + 1, up_odd)
        combine(2 * j, up_even)
        return carry

    lax.fori_loop(0, count // 2, two, 0)
    combine(count - 1, up_odd)
    for i in range(count):
        if i % 2 or i + 2 >= count:
            send(i, True, False)
    for i in range(count):
        send(i, False, True)


def lift(leaf, octant, interp, angle, place):
    rows, low = leaf.shape
    high = interp.shape[1]
    tile = 1024
    far = pl.BlockSpec(memory_space=pltpu.HBM)
    return pl.pallas_call(
        functools.partial(lift_kernel, place, tile),
        out_shape=jax.ShapeDtypeStruct((high // LANES, rows // 8, LANES), jnp.bfloat16),
        in_specs=[far, far, far, far],
        out_specs=far,
        scratch_shapes=[
            pltpu.SMEM(octant.shape, octant.dtype),
            pltpu.VMEM(leaf.shape, leaf.dtype),
            pltpu.VMEM(interp.shape, interp.dtype),
            pltpu.VMEM(angle.shape, angle.dtype),
            pltpu.VMEM((high // LANES, 8, LANES), jnp.float32),
            pltpu.VMEM((high // LANES, 8, LANES), jnp.float32),
            pltpu.VMEM((rows, tile), jnp.float32),
            pltpu.VMEM((rows, tile), jnp.float32),
            pltpu.VMEM((high // LANES, rows // 8, LANES), jnp.bfloat16),
            pltpu.SemaphoreType.DMA((high // tile,)),
            pltpu.SemaphoreType.DMA((3,)),
            pltpu.SemaphoreType.DMA((high // LANES,)),
        ],
        compiler_params=pltpu.CompilerParams(vmem_limit_bytes=24 * MIB),
        cost_estimate=pl.CostEstimate(
            flops=2 * rows * low * high, bytes_accessed=2 * low * high, transcendentals=0
        ),
        name="lift",
    )(*(pltpu.with_memory_space_constraint(x, pltpu.HBM) for x in (octant, leaf, interp, angle)))


def translate_kernel(linked, count, *refs):
    tables = refs[:count]
    received, factors, interp_far, angle_far = refs[count : count + 4]
    out, kept, cosines, sines, source, angle, ready = refs[count + 4 :]
    kept_copy = pltpu.make_async_copy(interp_far, kept, ready.at[0])
    angle_copy = pltpu.make_async_copy(angle_far, angle, ready.at[1])
    angle_copy.start()
    kept_copy.start()
    source[...] = received[...].astype(jnp.float32).reshape(source.shape)
    half = received.shape[1] // 2
    owned = tables[0].shape[0]
    side = lax.axis_index("box")
    for shift, table in enumerate(tables):
        base = lax.rem(side + shift, count) * owned

        def target(p, carry, table=table, base=base):
            real = imag = None
            for k in range(linked):
                code = table[p, k]
                row = pl.multiple_of(code & 0xFFFF, 2 * half)
                pair = code >> 16
                re = source[pl.ds(row, half), :]
                im = source[pl.ds(row + half, half), :]
                f_re = factors[pl.ds(pair, 1), :]
                f_im = factors[pl.ds(pair + 1, 1), :]
                a = f_re * re - f_im * im
                b = f_re * im + f_im * re
                real = a if real is None else real + a
                imag = b if imag is None else imag + b
            out[base + p] = jnp.concatenate([real, imag], 0).astype(out.dtype)
            return carry

        lax.fori_loop(0, owned, target, 0)
    angle_copy.wait()
    phases(angle, cosines, sines)
    kept_copy.wait()


def translate(tables, received, factors, interp, angle):
    parents, rows, width = received.shape
    linked = tables[0].shape[1]
    count = len(tables)
    high = interp.shape[1]
    smem = pl.BlockSpec(memory_space=pltpu.SMEM)
    vmem = pl.BlockSpec(memory_space=pltpu.VMEM)
    far = pl.BlockSpec(memory_space=pltpu.HBM)
    phase = pltpu.VMEM((high // LANES, 8, LANES), jnp.float32)
    return pl.pallas_call(
        functools.partial(translate_kernel, linked, count),
        out_shape=(
            pltpu.VMEM(received.shape, jnp.bfloat16),
            pltpu.VMEM(interp.shape, interp.dtype),
            phase,
            phase,
        ),
        in_specs=[smem] * count + [vmem, vmem, far, far],
        out_specs=(vmem,) * 4,
        scratch_shapes=[
            pltpu.VMEM((parents * rows, width), jnp.float32),
            pltpu.VMEM(angle.shape, angle.dtype),
            pltpu.SemaphoreType.DMA((2,)),
        ],
        compiler_params=pltpu.CompilerParams(vmem_limit_bytes=24 * MIB),
        cost_estimate=pl.CostEstimate(
            flops=8 * parents * linked * rows * width, bytes_accessed=4 << 20, transcendentals=0
        ),
        name="translate",
    )(
        *tables,
        received,
        factors,
        *(pltpu.with_memory_space_constraint(x, pltpu.HBM) for x in (interp, angle)),
    )


def descend_kernel(
    place, scale, tile, octant, incoming, kept, cosines, sines, out, even, odd, total
):
    low, high = kept.shape
    count = high // tile
    boxes = even.shape[0] // PAIR

    def shift(i, shifted):
        for lane in range(0, tile, LANES):
            block = i * (tile // LANES) + lane // LANES
            received = incoming[place(block)].astype(jnp.float32)
            for child in range(boxes):
                which = octant[child]
                cos = cosines[block, pl.ds(which, 1), :]
                sin = sines[block, pl.ds(which, 1), :]
                row = PAIR * (child // 8)
                in_re = received[row : row + EXCITE]
                in_im = received[row + EXCITE : row + PAIR]
                re = in_re * cos + in_im * sin
                im = in_im * cos - in_re * sin
                both = jnp.concatenate([re, im], 0).astype(jnp.bfloat16)
                shifted[PAIR * child : PAIR * (child + 1), lane : lane + LANES] = both

    def drop(i, shifted):
        total[...] += lax.dot_general(
            kept[:, chunk_of(i, tile)],
            shifted[...],
            (((1,), (1,)), ((), ())),
            preferred_element_type=jnp.float32,
        )

    def two(j, carry):
        drop(2 * j, even)
        shift(2 * j + 1, odd)
        drop(2 * j + 1, odd)
        shift(jnp.minimum(2 * j + 2, count - 1), even)
        return carry

    total[...] = jnp.zeros_like(total)
    shift(0, even)
    lax.fori_loop(0, count // 2, two, 0)
    out[...] = (total[...].T * scale).astype(out.dtype)


def descend(incoming, octant, kept, cosines, sines, place):
    low, high = kept.shape
    rows = incoming.shape[1] * 8
    tile = 512
    near = pl.BlockSpec(memory_space=pltpu.VMEM)
    return pl.pallas_call(
        functools.partial(descend_kernel, place, low / high, tile),
        out_shape=jax.ShapeDtypeStruct((rows, low), jnp.bfloat16),
        in_specs=[pl.BlockSpec(memory_space=pltpu.SMEM), near, near, near, near],
        out_specs=near,
        scratch_shapes=[
            pltpu.VMEM((rows, tile), jnp.bfloat16),
            pltpu.VMEM((rows, tile), jnp.bfloat16),
            pltpu.VMEM((low, rows), jnp.float32),
        ],
        compiler_params=pltpu.CompilerParams(vmem_limit_bytes=24 * MIB),
        cost_estimate=pl.CostEstimate(
            flops=2 * rows * low * high, bytes_accessed=2 * low * high, transcendentals=0
        ),
        name="descend",
    )(octant, incoming, kept, cosines, sines)


def local(leaf_patterns, octant, interp, shift_angle, partners, types, translators):
    boxes, pairs, excite, low = leaf_patterns.shape
    high = interp.shape[1]
    sides = lax.axis_size("box")
    groups = lax.axis_size("dir")
    devices = sides * groups
    axes = ("box", "dir")
    width = high // devices
    parents = boxes // 8
    rows = parents * PAIR
    direct = width == LANES

    def place(t):
        return lax.rem(t, sides) * groups + lax.div(t, sides) if direct else t

    outgoing = lift(leaf_patterns.reshape(-1, low), octant, interp, shift_angle, place)
    if not direct:
        outgoing = outgoing.transpose(1, 0, 2).reshape(rows, groups, sides, width)
        outgoing = outgoing.transpose(2, 1, 0, 3).reshape(devices, rows, width)
    received = lax.all_to_all(outgoing, axes, split_axis=0, concat_axis=0, tiled=True)
    received = received.reshape(devices * parents, PAIR, width)

    code = partners * PAIR | (types * 2 << 16)
    tables = [code] + [
        lax.ppermute(code, "box", [((s + shift) % sides, s) for s in range(sides)])
        for shift in range(1, sides)
    ]
    side = lax.axis_index("box")
    factors = lax.dynamic_slice_in_dim(translators, side * width, width, axis=2)
    incoming, kept, cosines, sines = translate(
        tables, received, factors.reshape(-1, width), interp, shift_angle
    )

    incoming = incoming.reshape(devices, rows, width)
    returned = lax.all_to_all(incoming, axes, split_axis=0, concat_axis=0, tiled=True)
    if not direct:
        returned = returned.reshape(sides, groups, rows, width).transpose(2, 1, 0, 3)
        returned = returned.reshape(rows, high // LANES, LANES).transpose(1, 0, 2)
    down = descend(returned, octant, kept, cosines, sines, place)
    return down.reshape(boxes, pairs, excite, low)


def solution(mesh):
    placed = (
        P(("box", "dir"), None, None, None),
        P(("box", "dir")),
        P(),
        P(),
        P("box", None),
        P("box", None),
        P(None, None, "dir"),
    )
    return jax.shard_map(
        local,
        mesh=mesh,
        in_specs=placed,
        out_specs=P(("box", "dir"), None, None, None),
        check_vma=False,
    )
```

time: 145 us -> 47 us (0.32)
  local copies, waits for them, and re-layouts: 71 us -> 0.38 us
  Pallas kernels: 0 us -> 16.6 us
  matrix products: 15.5 us -> 0 us
  other arithmetic: 14.5 us -> 0.01 us
  blocking collectives: 21.8 us -> 12.6 us
  loops' own time: 3.13 us -> 0 us
  waiting for transfers between devices: 9.83 us -> 8.01 us
  starting transfers between devices: 7.41 us -> 9.17 us
    gather x54 -> x0, local copies, waits for them, and re-layouts: 66 us -> none  [the longest x27 46.9 us: translate(): factor = jnp.take(translators, types[:, step], axis=0)]
    pallas_call x0 -> x3, Pallas kernels: none -> 16.6 us  [the longest x1 6.69 us: lift(): pl.pallas_call(functools.partial(lift_kernel, place, tile), out_shape=jax...]
    dot_general x4 -> x0, matrix products: 15.5 us -> none  [the longest x1 6.54 us: local(): lax.dot_general(shifted, interp, (((1,), (1,)), ((), ())), preferred_elem...]
    all_gather x1 -> x0, blocking collectives: 8.79 us -> none  [local(): every = lax.all_gather(regrouped, 'box', axis=0, tiled=True)]
    add x27 -> x0, other arithmetic: 4.5 us -> none  [translate(): return total + jnp.stack([real_part, imag_part], 1)]
    all_to_all x1, waiting for transfers between devices: 9.83 us -> 6.15 us  [local(): lax.all_to_all(outgoing, axes, split_axis=0, concat_axis=0, tiled=True)]
    convert_element_type x29 -> x0, other arithmetic: 3.2 us -> none  [the longest x27 2.96 us: translate(): source = jnp.take(every, partners[:, step], axis=0).reshape(owned, 2, exc...]
    another operation x1 -> x0, loops' own time: 3.13 us -> none  [local(): summed = lax.fori_loop(0, linked, translate, zero)]
  transfers between devices with their start and end apart: 1 -> 2, of which waited for: 1 -> 2; matrix products, arithmetic and copies ran while one was open for 0% -> 1% of each run, Pallas kernels for 0% -> 0%
where the time goes in v1:
time: 47 us; the launch traced here: 46.8 us
  Pallas kernels  16.6 us (35%)
  blocking collectives  12.6 us (27%)
  starting transfers between devices  9.17 us (20%)
  waiting for transfers between devices  8.01 us (17%)
    all_to_all x1, blocking collectives, local(): lax.all_to_all(incoming, axes, split_axis=0, concat_axis=0, tiled=True)  12.6 us
    all_to_all x1, starting transfers between devices, local(): lax.all_to_all(outgoing, axes, split_axis=0, concat_axis=0, tiled=True)  7.34 us
    pallas_call x1, Pallas kernels, lift(): pl.pallas_call(functools.partial(lift_kernel, place, tile), out_shape=jax...  6.69 us
    all_to_all x1, waiting for transfers between devices, local(): lax.all_to_all(outgoing, axes, split_axis=0, concat_axis=0, tiled=True)  6.15 us
    pallas_call x1, Pallas kernels, descend(): pl.pallas_call(functools.partial(descend_kernel, place, low / high, tile)...  5.15 us
    pallas_call x1, Pallas kernels, translate(): pl.pallas_call(functools.partial(translate_kernel, linked, count), out_sh...  4.73 us
    ppermute x1, waiting for transfers between devices, local(): lax.ppermute(code, 'box', [((s + shift) % sides, s) for s in range(sides)])  1.86 us
    ppermute x1, starting transfers between devices, local(): lax.ppermute(code, 'box', [((s + shift) % sides, s) for s in range(sides)])  1.83 us
  transfers between devices with their start and end apart: 2, of which 2 were waited for; matrix products, arithmetic and copies ran while one was open for 1% of the time, Pallas kernels for 0%

profile of v1, /device:TPU:0, one launch (start us, length us, event | category | flops | bytes accessed | tf_op | source)
XLA Modules:
  0.0 46.8 jit_solution(15318130134097791336)
XLA Ops:
  0.0 0.0 copy-start
  0.0 0.0 copy-start.2
  0.0 0.0 copy-start.3
  0.0 0.0 copy-start.1
  0.0 6.7 %lift.1 = bf16[32,32,128]{2,1,0:T(8,128)(2,1)} custom-call(s32[16]{0:T(128)} %octant.1, bf16[256,1024]{1,0:T(8,128)(2,1)} %bitcast.6, bf16[1024,4096]{1,0:T(8,128)(2,1)} %refs_4_.1, f32[8,4096]{1,0:T(8,128)} %refs_5_.1), custom_call_target="tpu_custom_call" | custom-call | flops 2147483648 | bytes 8388608 | tf_op jit(solution)/shard_map/lift/pallas_call | solution.py:136
  6.7 7.3 %all-to-all-start = ((bf16[32,32,128]{2,1,0:T(8,128)(2,1)}), bf16[32,32,128]{2,1,0:T(8,128)(2,1)S(1)}, u32[]{:S(2)}, u32[]{:S(2)}) async-start(bf16[32,32,128]{2,1,0:T(8,128)(2,1)} %lift.1), calls=%async_computation | async-start | bytes 524288 | tf_op jit(solution)/shard_map/all_to_all | solution.py:324
  14.1 0.0 copy-done.2
  14.1 0.0 copy-done.3
  14.1 1.8 %collective-permute-start = (s32[32,27]{1,0:T(8,128)S(1)}, s32[32,27]{1,0:T(8,128)S(1)}, u32[]{:S(2)}, u32[]{:S(2)}) collective-permute-start(s32[32,27]{1,0:T(8,128)S(1)} %shift-left_or_fusion.refs_0_), channel_id=1, source_target_pairs={{16,0},{0,16},{17,1},{1,17},{18,2},{2,18},{19,3},{3,19},{20,4},{4,... | collective-permute-start | bytes 10376 | tf_op jit(solution)/shard_map/ppermute | solution.py:329
  15.9 0.0 copy-done
  15.9 0.1 constant_dynamic-slice_fusion
  16.1 0.2 reshape.17.refs_3_
  16.3 1.9 %collective-permute-done.refs_1_ = s32[32,27]{1,0:T(8,128)S(1)} collective-permute-done((s32[32,27]{1,0:T(8,128)S(1)}, s32[32,27]{1,0:T(8,128)S(1)}, u32[]{:S(2)}, u32[]{:S(2)}) %collective-permute-start) | collective-permute-done | bytes 3488 | tf_op jit(solution)/shard_map/ppermute | solution.py:329
  18.2 6.1 %all-to-all-done = bf16[32,32,128]{2,1,0:T(8,128)(2,1)S(1)} async-done(((bf16[32,32,128]{2,1,0:T(8,128)(2,1)}), bf16[32,32,128]{2,1,0:T(8,128)(2,1)S(1)}, u32[]{:S(2)}, u32[]{:S(2)}) %all-to-all-start) | async-done | bytes 262176 | tf_op jit(solution)/shard_map/all_to_all | solution.py:324
  24.3 4.7 %translate.1 = (bf16[64,16,128]{2,1,0:T(8,128)(2,1)S(1)}, bf16[1024,4096]{1,0:T(8,128)(2,1)S(1)}, f32[32,8,128]{2,1,0:T(8,128)S(1)}, f32[32,8,128]{2,1,0:T(8,128)S(1)}) custom-call(s32[32,27]{1,0:T(8,128)S(1)} %shift-left_or_fusion.refs_0_, s32[32,27]{1,0:T(8,128)S(1)} %collective-permute-done.refs_1_, bf16[64,16,128]{2,1,0:T(8,128)(2,1)S(1)} %bitcast.4, ...), custom_call_target="tpu_custom_call" | custom-call | flops 28311552 | bytes 4194304 | tf_op jit(solution)/shard_map/translate/pallas_call | solution.py:210
  29.1 12.6 %all_to_all.10.incoming = bf16[32,32,128]{2,1,0:T(8,128)(2,1)S(1)} all-to-all(bf16[32,32,128]{2,1,0:T(8,128)(2,1)S(1)} %bitcast.5), channel_id=1, replica_groups=mesh['box'=2,'dir'=16] {'box','dir'}, dimensions={0} | all-to-all | bytes 524288 | tf_op jit(solution)/shard_map/all_to_all | solution.py:339
  41.7 0.0 copy-done.1
  41.7 5.1 %descend.1 = bf16[256,1024]{1,0:T(8,128)(2,1)} custom-call(s32[16]{0:T(128)S(1)} %copy-done.1, bf16[32,32,128]{2,1,0:T(8,128)(2,1)S(1)} %all_to_all.10.incoming, bf16[1024,4096]{1,0:T(8,128)(2,1)S(1)} %get-tuple-element.10.kept, f32[32,8,128]{2,1,0:T(8,128)S(1)} %get-tuple-element.11.cosines, f32[32,8,128]{2,1,0:T(8,128)S(1)} %get-tuple-element.12.sines), custom_call_target="tpu_custom_call" | custom-call | flops 2147483648 | bytes 8388608 | tf_op jit(solution)/shard_map/descend/pallas_call | solution.py:287
  (1 shorter events, 0.0 us)
Async XLA Ops:
  0.0 15.9 %copy-start = (f32[343,2,256]{2,1,0:T(2,128)S(1)}, f32[343,2,256]{2,1,0:T(2,128)}, u32[]{:S(2)}) copy-start(f32[343,2,256]{2,1,0:T(2,128)} %param.13) | copy-start | bytes 2107396
  0.0 14.1 %copy-start.2 = (s32[32,27]{1,0:T(8,128)S(1)}, s32[32,27]{1,0:T(8,128)}, u32[]{:S(2)}) copy-start(s32[32,27]{1,0:T(8,128)} %param.12) | copy-start | bytes 10372
  0.0 14.1 %copy-start.3 = (s32[32,27]{1,0:T(8,128)S(1)}, s32[32,27]{1,0:T(8,128)}, u32[]{:S(2)}) copy-start(s32[32,27]{1,0:T(8,128)} %param.11) | copy-start | bytes 10372
  0.0 41.6 %copy-start.1 = (s32[16]{0:T(128)S(1)}, s32[16]{0:T(128)}, u32[]{:S(2)}) copy-start(s32[16]{0:T(128)} %octant.1) | copy-start | bytes 196
  6.7 17.6 %all-to-all-start = ((bf16[32,32,128]{2,1,0:T(8,128)(2,1)}), bf16[32,32,128]{2,1,0:T(8,128)(2,1)S(1)}, u32[]{:S(2)}, u32[]{:S(2)}) async-start(bf16[32,32,128]{2,1,0:T(8,128)(2,1)} %lift.1), calls=%async_computation | async-start | bytes 524288 | tf_op jit(solution)/shard_map/all_to_all | solution.py:324
  14.1 4.1 %collective-permute-start = (s32[32,27]{1,0:T(8,128)S(1)}, s32[32,27]{1,0:T(8,128)S(1)}, u32[]{:S(2)}, u32[]{:S(2)}) collective-permute-start(s32[32,27]{1,0:T(8,128)S(1)} %shift-left_or_fusion.refs_0_), channel_id=1, source_target_pairs={{16,0},{0,16},{17,1},{1,17},{18,2},{2,18},{19,3},{3,19},{20,4},{4,... | collective-permute-start | bytes 10376 | tf_op jit(solution)/shard_map/ppermute | solution.py:329

commit v2 on v1

--- a/solution.py
+++ b/solution.py
@@ -12,6 +12,7 @@
 PAIR = 2 * EXCITE
 MIB = 1 << 20
 AHEAD = 2
+TILE3 = 1024
 
 
 def sincos(x):
@@ -51,7 +52,7 @@
 
 
 def lift_kernel(
-    place, tile, octant_far, leaf_far, interp_far, angle_far, out_far,
+    place, tile, octant_far, leaf_far, interp_far, angle_far, out_far, cosines_far, sines_far,
     octant, leaf, interp, angle, cosines, sines, up_even, up_odd, out, arrived, ready, sent,
 ):
     low, high = interp.shape
@@ -68,6 +69,10 @@
         column_copy(interp_far, interp, arrived, tile, i).start()
     angle_copy.wait()
     phases(angle, cosines, sines)
+    cosines_copy = pltpu.make_async_copy(cosines, cosines_far, ready.at[3])
+    sines_copy = pltpu.make_async_copy(sines, sines_far, ready.at[4])
+    cosines_copy.start()
+    sines_copy.start()
     octant_copy.wait()
     leaf_copy.wait()
 
@@ -126,6 +131,8 @@
             send(i, True, False)
     for i in range(count):
         send(i, False, True)
+    cosines_copy.wait()
+    sines_copy.wait()
 
 
 def lift(leaf, octant, interp, angle, place):
@@ -133,11 +140,16 @@
     high = interp.shape[1]
     tile = 1024
     far = pl.BlockSpec(memory_space=pltpu.HBM)
+    phase = pltpu.HBM((high // LANES, 8, LANES), jnp.float32)
     return pl.pallas_call(
         functools.partial(lift_kernel, place, tile),
-        out_shape=jax.ShapeDtypeStruct((high // LANES, rows // 8, LANES), jnp.bfloat16),
+        out_shape=(
+            jax.ShapeDtypeStruct((high // LANES, rows // 8, LANES), jnp.bfloat16),
+            phase,
+            phase,
+        ),
         in_specs=[far, far, far, far],
-        out_specs=far,
+        out_specs=(far, far, far),
         scratch_shapes=[
             pltpu.SMEM(octant.shape, octant.dtype),
             pltpu.VMEM(leaf.shape, leaf.dtype),
@@ -149,7 +161,7 @@
             pltpu.VMEM((rows, tile), jnp.float32),
             pltpu.VMEM((high // LANES, rows // 8, LANES), jnp.bfloat16),
             pltpu.SemaphoreType.DMA((high // tile,)),
-            pltpu.SemaphoreType.DMA((3,)),
+            pltpu.SemaphoreType.DMA((5,)),
             pltpu.SemaphoreType.DMA((high // LANES,)),
         ],
         compiler_params=pltpu.CompilerParams(vmem_limit_bytes=24 * MIB),
@@ -160,16 +172,25 @@
     )(*(pltpu.with_memory_space_constraint(x, pltpu.HBM) for x in (octant, leaf, interp, angle)))
 
 
-def translate_kernel(linked, count, *refs):
+def grid_slot(index, bits):
+    slot = 0
+    for bit in range(bits):
+        slot = slot + ((index >> bit) & 1) * ((49, 7, 1)[bit % 3] << (bit // 3))
+    return slot
+
+
+def translate_grid_kernel(linked, bits, count, *refs):
     tables = refs[:count]
-    received, factors, interp_far, angle_far = refs[count : count + 4]
-    out, kept, cosines, sines, source, angle, ready = refs[count + 4 :]
-    kept_copy = pltpu.make_async_copy(interp_far, kept, ready.at[0])
-    angle_copy = pltpu.make_async_copy(angle_far, angle, ready.at[1])
-    angle_copy.start()
-    kept_copy.start()
-    source[...] = received[...].astype(jnp.float32).reshape(source.shape)
-    half = received.shape[1] // 2
+    received, factors, out, source = refs[count:]
+    lead = 3 * (49 + 7 + 1) * EXCITE
+    last = grid_slot(received.shape[0] - 1, bits) * EXCITE
+    imag_at = lead + last + EXCITE
+    span = source.shape[0] - last
+    for parent in range(received.shape[0]):
+        both = received[parent].astype(jnp.float32)
+        row = lead + grid_slot(parent, bits) * EXCITE
+        source[row : row + EXCITE, :] = both[:EXCITE]
+        source[imag_at + row : imag_at + row + EXCITE, :] = both[EXCITE:]
     owned = tables[0].shape[0]
     side = lax.axis_index("box")
     for shift, table in enumerate(tables):
@@ -177,12 +198,41 @@
 
         def target(p, carry, table=table, base=base):
             real = imag = None
+            start = pl.multiple_of(table[p, linked], EXCITE)
+            view = source.at[pl.ds(start, span)]
+            for k in range(linked):
+                row = pl.multiple_of(table[p, k], EXCITE)
+                re = view[pl.ds(row, EXCITE), :]
+                im = view[pl.ds(row + imag_at, EXCITE), :]
+                f_re = factors[pl.ds(row, 1), :]
+                f_im = factors[pl.ds(row + 1, 1), :]
+                a = f_re * re - f_im * im
+                b = f_re * im + f_im * re
+                real = a if real is None else real + a
+                imag = b if imag is None else imag + b
+            out[base + p] = jnp.concatenate([real, imag], 0).astype(out.dtype)
+            return carry
+
+        lax.fori_loop(0, owned, target, 0, unroll=2)
+
+
+def translate_kernel(linked, count, *refs):
+    tables = refs[:count]
+    received, factors, out, source = refs[count:]
+    source[...] = received[...].astype(jnp.float32).reshape(source.shape)
+    owned = tables[0].shape[0]
+    side = lax.axis_index("box")
+    for shift, table in enumerate(tables):
+        base = lax.rem(side + shift, count) * owned
+
+        def target(p, carry, table=table, base=base):
+            real = imag = None
             for k in range(linked):
                 code = table[p, k]
-                row = pl.multiple_of(code & 0xFFFF, 2 * half)
-                pair = code >> 16
-                re = source[pl.ds(row, half), :]
-                im = source[pl.ds(row + half, half), :]
+                row = pl.multiple_of(code & 0xFFFF, PAIR)
+                pair = pl.multiple_of(code >> 16, EXCITE)
+                re = source[pl.ds(row, EXCITE), :]
+                im = source[pl.ds(row + EXCITE, EXCITE), :]
                 f_re = factors[pl.ds(pair, 1), :]
                 f_im = factors[pl.ds(pair + 1, 1), :]
                 a = f_re * re - f_im * im
@@ -193,54 +243,41 @@
             return carry
 
         lax.fori_loop(0, owned, target, 0)
-    angle_copy.wait()
-    phases(angle, cosines, sines)
-    kept_copy.wait()
-
-
-def translate(tables, received, factors, interp, angle):
+
+
+def translate(tables, received, factors, linked, bits):
     parents, rows, width = received.shape
-    linked = tables[0].shape[1]
     count = len(tables)
-    high = interp.shape[1]
     smem = pl.BlockSpec(memory_space=pltpu.SMEM)
     vmem = pl.BlockSpec(memory_space=pltpu.VMEM)
-    far = pl.BlockSpec(memory_space=pltpu.HBM)
-    phase = pltpu.VMEM((high // LANES, 8, LANES), jnp.float32)
+    if bits is None:
+        kernel = functools.partial(translate_kernel, linked, count)
+        source = parents * rows
+    else:
+        kernel = functools.partial(translate_grid_kernel, linked, bits, count)
+        source = (2 * grid_slot(parents - 1, bits) + 2 + 9 * (49 + 7 + 1)) * EXCITE
     return pl.pallas_call(
-        functools.partial(translate_kernel, linked, count),
-        out_shape=(
-            pltpu.VMEM(received.shape, jnp.bfloat16),
-            pltpu.VMEM(interp.shape, interp.dtype),
-            phase,
-            phase,
-        ),
-        in_specs=[smem] * count + [vmem, vmem, far, far],
-        out_specs=(vmem,) * 4,
-        scratch_shapes=[
-            pltpu.VMEM((parents * rows, width), jnp.float32),
-            pltpu.VMEM(angle.shape, angle.dtype),
-            pltpu.SemaphoreType.DMA((2,)),
-        ],
-        compiler_params=pltpu.CompilerParams(vmem_limit_bytes=24 * MIB),
-        cost_estimate=pl.CostEstimate(
-            flops=8 * parents * linked * rows * width, bytes_accessed=4 << 20, transcendentals=0
-        ),
+        kernel,
+        out_shape=jax.ShapeDtypeStruct(received.shape, jnp.bfloat16),
+        in_specs=[smem] * count + [vmem, vmem],
+        out_specs=vmem,
+        scratch_shapes=[pltpu.VMEM((source, width), jnp.float32)],
+        compiler_params=pltpu.CompilerParams(vmem_limit_bytes=12 * MIB),
+        cost_estimate=pl.CostEstimate(flops=4 << 30, bytes_accessed=4 << 20, transcendentals=0),
         name="translate",
-    )(
-        *tables,
-        received,
-        factors,
-        *(pltpu.with_memory_space_constraint(x, pltpu.HBM) for x in (interp, angle)),
-    )
+    )(*tables, received, factors)
 
 
 def descend_kernel(
-    place, scale, tile, octant, incoming, kept, cosines, sines, out, even, odd, total
+    place, scale, tile, octant_far, incoming, interp, cosines, sines, out_far,
+    octant, even, odd, total, out, sent, ready,
 ):
-    low, high = kept.shape
+    low, high = interp.shape
     count = high // tile
     boxes = even.shape[0] // PAIR
+    octant_copy = pltpu.make_async_copy(octant_far, octant, ready)
+    octant_copy.start()
+    octant_copy.wait()
 
     def shift(i, shifted):
         for lane in range(0, tile, LANES):
@@ -258,48 +295,56 @@
                 both = jnp.concatenate([re, im], 0).astype(jnp.bfloat16)
                 shifted[PAIR * child : PAIR * (child + 1), lane : lane + LANES] = both
 
-    def drop(i, shifted):
-        total[...] += lax.dot_general(
-            kept[:, chunk_of(i, tile)],
-            shifted[...],
+    halves = (even, odd)
+    shift(0, even)
+    for i in range(count):
+        part = lax.dot_general(
+            interp[:, i * tile : (i + 1) * tile],
+            halves[i % 2][...],
             (((1,), (1,)), ((), ())),
             preferred_element_type=jnp.float32,
         )
-
-    def two(j, carry):
-        drop(2 * j, even)
-        shift(2 * j + 1, odd)
-        drop(2 * j + 1, odd)
-        shift(jnp.minimum(2 * j + 2, count - 1), even)
-        return carry
-
-    total[...] = jnp.zeros_like(total)
-    shift(0, even)
-    lax.fori_loop(0, count // 2, two, 0)
-    out[...] = (total[...].T * scale).astype(out.dtype)
-
-
-def descend(incoming, octant, kept, cosines, sines, place):
-    low, high = kept.shape
+        total[...] = part if i == 0 else total[...] + part
+        if i + 1 < count:
+            shift(i + 1, halves[(i + 1) % 2])
+    step = low // sent.shape[0]
+    copies = []
+    for i in range(sent.shape[0]):
+        columns = pl.ds(i * step, step)
+        out[:, columns] = (total[columns, :].T * scale).astype(out.dtype)
+        copies.append(pltpu.make_async_copy(out.at[:, columns], out_far.at[:, columns], sent.at[i]))
+        copies[-1].start()
+    for copy in copies:
+        copy.wait()
+
+
+def descend(incoming, octant, interp, cosines, sines, place):
+    low, high = interp.shape
     rows = incoming.shape[1] * 8
-    tile = 512
+    tile = TILE3
     near = pl.BlockSpec(memory_space=pltpu.VMEM)
+    far = pl.BlockSpec(memory_space=pltpu.HBM)
+    octant = pltpu.with_memory_space_constraint(octant, pltpu.HBM)
     return pl.pallas_call(
         functools.partial(descend_kernel, place, low / high, tile),
         out_shape=jax.ShapeDtypeStruct((rows, low), jnp.bfloat16),
-        in_specs=[pl.BlockSpec(memory_space=pltpu.SMEM), near, near, near, near],
-        out_specs=near,
+        in_specs=[far, near, near, near, near],
+        out_specs=far,
         scratch_shapes=[
+            pltpu.SMEM(octant.shape, octant.dtype),
             pltpu.VMEM((rows, tile), jnp.bfloat16),
             pltpu.VMEM((rows, tile), jnp.bfloat16),
             pltpu.VMEM((low, rows), jnp.float32),
+            pltpu.VMEM((rows, low), jnp.bfloat16),
+            pltpu.SemaphoreType.DMA((4,)),
+            pltpu.SemaphoreType.DMA(()),
         ],
-        compiler_params=pltpu.CompilerParams(vmem_limit_bytes=24 * MIB),
+        compiler_params=pltpu.CompilerParams(vmem_limit_bytes=12 * MIB),
         cost_estimate=pl.CostEstimate(
             flops=2 * rows * low * high, bytes_accessed=2 * low * high, transcendentals=0
         ),
         name="descend",
-    )(octant, incoming, kept, cosines, sines)
+    )(octant, incoming, interp, cosines, sines)
 
 
 def local(leaf_patterns, octant, interp, shift_angle, partners, types, translators):
@@ -317,30 +362,38 @@
     def place(t):
         return lax.rem(t, sides) * groups + lax.div(t, sides) if direct else t
 
-    outgoing = lift(leaf_patterns.reshape(-1, low), octant, interp, shift_angle, place)
+    outgoing, cosines, sines = lift(leaf_patterns.reshape(-1, low), octant, interp, shift_angle, place)
     if not direct:
         outgoing = outgoing.transpose(1, 0, 2).reshape(rows, groups, sides, width)
         outgoing = outgoing.transpose(2, 1, 0, 3).reshape(devices, rows, width)
     received = lax.all_to_all(outgoing, axes, split_axis=0, concat_axis=0, tiled=True)
     received = received.reshape(devices * parents, PAIR, width)
 
-    code = partners * PAIR | (types * 2 << 16)
+    side = lax.axis_index("box")
+    owned, linked = types.shape
+    bits = (devices * parents - 1).bit_length()
+    extent = 1 << (bits + 2) // 3
+    if extent <= 7:
+        own = side * owned + jnp.arange(owned, dtype=jnp.int32)
+        start = grid_slot(own, bits)
+        code = jnp.concatenate([types, start[:, None]], 1) * EXCITE
+    else:
+        bits = None
+        code = partners * PAIR | (types * EXCITE << 16)
     tables = [code] + [
         lax.ppermute(code, "box", [((s + shift) % sides, s) for s in range(sides)])
         for shift in range(1, sides)
     ]
-    side = lax.axis_index("box")
     factors = lax.dynamic_slice_in_dim(translators, side * width, width, axis=2)
-    incoming, kept, cosines, sines = translate(
-        tables, received, factors.reshape(-1, width), interp, shift_angle
-    )
+    factors = jnp.pad(factors, ((0, 0), (0, EXCITE - 2), (0, 0))).reshape(-1, width)
+    incoming = translate(tables, received, factors, linked, bits)
 
     incoming = incoming.reshape(devices, rows, width)
     returned = lax.all_to_all(incoming, axes, split_axis=0, concat_axis=0, tiled=True)
     if not direct:
         returned = returned.reshape(sides, groups, rows, width).transpose(2, 1, 0, 3)
         returned = returned.reshape(rows, high // LANES, LANES).transpose(1, 0, 2)
-    down = descend(returned, octant, kept, cosines, sines, place)
+    down = descend(returned, octant, interp, cosines, sines, place)
     return down.reshape(boxes, pairs, excite, low)
 
 

time: 47 us -> 44.8 us (0.953)
  Pallas kernels: 16.6 us -> 14.3 us
    pallas_call x2, Pallas kernels: 11.4 us -> 10.1 us  [the longest x1 6.73 us: lift(): pl.pallas_call(functools.partial(lift_kernel, place, tile), out_shape=(ja...]
    pallas_call x1, Pallas kernels: 5.15 us -> 4.19 us  [descend(): pl.pallas_call(functools.partial(descend_kernel, place, low / high, tile)...]
where the time goes in v2:
time: 44.8 us; the launch traced here: 44.6 us
  Pallas kernels  14.3 us (32%)
  blocking collectives  12.6 us (28%)
  starting transfers between devices  9.11 us (20%)
  waiting for transfers between devices  8.13 us (18%)
    all_to_all x1, blocking collectives, local(): lax.all_to_all(incoming, axes, split_axis=0, concat_axis=0, tiled=True)  12.6 us
    all_to_all x1, starting transfers between devices, local(): lax.all_to_all(outgoing, axes, split_axis=0, concat_axis=0, tiled=True)  7.33 us
    pallas_call x1, Pallas kernels, lift(): pl.pallas_call(functools.partial(lift_kernel, place, tile), out_shape=(ja...  6.73 us
    all_to_all x1, waiting for transfers between devices, local(): lax.all_to_all(outgoing, axes, split_axis=0, concat_axis=0, tiled=True)  6.15 us
    pallas_call x1, Pallas kernels, descend(): pl.pallas_call(functools.partial(descend_kernel, place, low / high, tile)...  4.19 us
    pallas_call x1, Pallas kernels, translate(): pl.pallas_call(kernel, out_shape=jax.ShapeDtypeStruct(received.shape, jnp...  3.41 us
    ppermute x1, waiting for transfers between devices, local(): lax.ppermute(code, 'box', [((s + shift) % sides, s) for s in range(sides)])  1.98 us
    ppermute x1, starting transfers between devices, local(): lax.ppermute(code, 'box', [((s + shift) % sides, s) for s in range(sides)])  1.77 us
  transfers between devices with their start and end apart: 2, of which 2 were waited for; matrix products, arithmetic and copies ran while one was open for 1% of the time, Pallas kernels for 0%

profile of v2, /device:TPU:0, one launch (start us, length us, event | category | flops | bytes accessed | tf_op | source)
XLA Modules:
  0.0 44.6 jit_solution(12616626384788343063)
XLA Ops:
  0.0 0.0 copy-start
  0.0 0.0 copy-start.3
  0.0 6.7 %lift.1 = (bf16[32,32,128]{2,1,0:T(8,128)(2,1)}, f32[32,8,128]{2,1,0:T(8,128)}, f32[32,8,128]{2,1,0:T(8,128)}) custom-call(s32[16]{0:T(128)} %octant_far.3, bf16[256,1024]{1,0:T(8,128)(2,1)} %bitcast.10, bf16[1024,4096]{1,0:T(8,128)(2,1)} %interp.1, f32[8,4096]{1,0:T(8,128)} %angle_far.1), custom_call_target="tpu_custom_call" | custom-call | flops 2147483648 | bytes 8388608 | tf_op jit(solution)/shard_map/lift/pallas_call | solution.py:144
  6.7 7.3 %all-to-all-start = ((bf16[32,32,128]{2,1,0:T(8,128)(2,1)}), bf16[32,32,128]{2,1,0:T(8,128)(2,1)S(1)}, u32[]{:S(2)}, u32[]{:S(2)}) async-start(bf16[32,32,128]{2,1,0:T(8,128)(2,1)} %get-tuple-element.8), calls=%async_computation | async-start | bytes 524288 | tf_op jit(solution)/shard_map/all_to_all | solution.py:369
  14.1 0.0 copy-done.3
  14.1 0.1 add_multiply_fusion.refs_0_
  14.2 1.8 %collective-permute-start = (s32[32,28]{1,0:T(8,128)S(1)}, s32[32,28]{1,0:T(8,128)S(1)}, u32[]{:S(2)}, u32[]{:S(2)}) collective-permute-start(s32[32,28]{1,0:T(8,128)S(1)} %add_multiply_fusion.refs_0_), channel_id=1, source_target_pairs={{16,0},{0,16},{17,1},{1,17},{18,2},{2,18},{19,3},{3,19},{20,4},{4,... | collective-permute-start | bytes 10760 | tf_op jit(solution)/shard_map/ppermute | solution.py:384
  16.0 0.0 copy-done
  16.0 0.1 constant_dynamic-slice_fusion
  16.1 0.1 pad_bitcast_fusion.refs_3_
  16.2 2.0 %collective-permute-done.refs_1_ = s32[32,28]{1,0:T(8,128)S(1)} collective-permute-done((s32[32,28]{1,0:T(8,128)S(1)}, s32[32,28]{1,0:T(8,128)S(1)}, u32[]{:S(2)}, u32[]{:S(2)}) %collective-permute-start) | collective-permute-done | bytes 3616 | tf_op jit(solution)/shard_map/ppermute | solution.py:384
  18.2 6.1 %all-to-all-done = bf16[32,32,128]{2,1,0:T(8,128)(2,1)S(1)} async-done(((bf16[32,32,128]{2,1,0:T(8,128)(2,1)}), bf16[32,32,128]{2,1,0:T(8,128)(2,1)S(1)}, u32[]{:S(2)}, u32[]{:S(2)}) %all-to-all-start) | async-done | bytes 262176 | tf_op jit(solution)/shard_map/all_to_all | solution.py:369
  24.3 0.0 slice-start
  24.3 0.0 slice-start.1
  24.3 0.0 copy-start.1
  24.3 0.0 copy-start.2
  24.3 3.4 %translate.1 = bf16[64,16,128]{2,1,0:T(8,128)(2,1)S(1)} custom-call(s32[32,28]{1,0:T(8,128)S(1)} %add_multiply_fusion.refs_0_, s32[32,28]{1,0:T(8,128)S(1)} %collective-permute-done.refs_1_, bf16[64,16,128]{2,1,0:T(8,128)(2,1)S(1)} %bitcast.8, f32[2744,128]{1,0:T(8,128)S(1)} %pad_bitcast_fusion.refs_3_), custom_call_target="tpu_custom_call" | custom-call | flops 4294967296 | bytes 4194304 | tf_op jit(solution)/shard_map/translate/pallas_call | solution.py:259
  27.8 12.6 %all_to_all.10.incoming = bf16[32,32,128]{2,1,0:T(8,128)(2,1)S(1)} all-to-all(bf16[32,32,128]{2,1,0:T(8,128)(2,1)S(1)} %bitcast.9), channel_id=1, replica_groups=mesh['box'=2,'dir'=16] {'box','dir'}, dimensions={0} | all-to-all | bytes 524288 | tf_op jit(solution)/shard_map/all_to_all | solution.py:392
  40.4 0.0 slice-done
  40.4 0.0 slice-done.1
  40.4 0.0 copy-done.1
  40.4 0.0 copy-done.2
  40.4 4.2 %descend.1 = bf16[256,1024]{1,0:T(8,128)(2,1)} custom-call(s32[16]{0:T(128)} %octant_far.3, bf16[32,32,128]{2,1,0:T(8,128)(2,1)S(1)} %all_to_all.10.incoming, bf16[1024,4096]{1,0:T(8,128)(2,1)S(1)} %bitcast.7, f32[32,8,128]{2,1,0:T(8,128)S(1)} %copy-done.1, f32[32,8,128]{2,1,0:T(8,128)S(1)} %copy-done.2), custom_call_target="tpu_custom_call" | custom-call | flops 2147483648 | bytes 8388608 | tf_op jit(solution)/shard_map/descend/pallas_call | solution.py:328
  (2 shorter events, 0.0 us)
Async XLA Ops:
  0.0 16.0 %copy-start = (f32[343,2,256]{2,1,0:T(2,128)S(1)}, f32[343,2,256]{2,1,0:T(2,128)}, u32[]{:S(2)}) copy-start(f32[343,2,256]{2,1,0:T(2,128)} %param.12) | copy-start | bytes 2107396
  0.0 14.1 %copy-start.3 = (s32[32,27]{1,0:T(8,128)S(1)}, s32[32,27]{1,0:T(8,128)}, u32[]{:S(2)}) copy-start(s32[32,27]{1,0:T(8,128)} %param.11) | copy-start | bytes 10372
  6.7 17.6 %all-to-all-start = ((bf16[32,32,128]{2,1,0:T(8,128)(2,1)}), bf16[32,32,128]{2,1,0:T(8,128)(2,1)S(1)}, u32[]{:S(2)}, u32[]{:S(2)}) async-start(bf16[32,32,128]{2,1,0:T(8,128)(2,1)} %get-tuple-element.8), calls=%async_computation | async-start | bytes 524288 | tf_op jit(solution)/shard_map/all_to_all | solution.py:369
  14.2 4.0 %collective-permute-start = (s32[32,28]{1,0:T(8,128)S(1)}, s32[32,28]{1,0:T(8,128)S(1)}, u32[]{:S(2)}, u32[]{:S(2)}) collective-permute-start(s32[32,28]{1,0:T(8,128)S(1)} %add_multiply_fusion.refs_0_), channel_id=1, source_target_pairs={{16,0},{0,16},{17,1},{1,17},{18,2},{2,18},{19,3},{3,19},{20,4},{4,... | collective-permute-start | bytes 10760 | tf_op jit(solution)/shard_map/ppermute | solution.py:384
  24.3 16.0 %slice-start = ((s8[8388608]{0:T(1024)(128)(4,1)}), s8[4194304]{0:T(1024)(128)(4,1)S(1)}, s32[]{:S(2)}) async-start(s8[8388608]{0:T(1024)(128)(4,1)} %bitcast.6), calls=%async_computation.2 | async-start | bytes 8388608
  24.3 16.0 %slice-start.1 = ((s8[8388608]{0:T(1024)(128)(4,1)}), s8[4194304]{0:T(1024)(128)(4,1)S(1)}, s32[]{:S(2)}) async-start(s8[8388608]{0:T(1024)(128)(4,1)} %bitcast.6), calls=%async_computation.3 | async-start | bytes 8388608
  24.3 16.0 %copy-start.1 = (f32[32,8,128]{2,1,0:T(8,128)S(1)}, f32[32,8,128]{2,1,0:T(8,128)}, u32[]{:S(2)}) copy-start(f32[32,8,128]{2,1,0:T(8,128)} %get-tuple-element.9.cosines) | copy-start | bytes 393220
  24.3 16.0 %copy-start.2 = (f32[32,8,128]{2,1,0:T(8,128)S(1)}, f32[32,8,128]{2,1,0:T(8,128)}, u32[]{:S(2)}) copy-start(f32[32,8,128]{2,1,0:T(8,128)} %get-tuple-element.10.sines) | copy-start | bytes 393220

commit v3 on v2

--- a/solution.py
+++ b/solution.py
@@ -12,7 +12,7 @@
 PAIR = 2 * EXCITE
 MIB = 1 << 20
 AHEAD = 2
-TILE3 = 1024
+TILE3 = 512
 
 
 def sincos(x):
@@ -213,7 +213,7 @@
             out[base + p] = jnp.concatenate([real, imag], 0).astype(out.dtype)
             return carry
 
-        lax.fori_loop(0, owned, target, 0, unroll=2)
+        lax.fori_loop(0, owned, target, 0, unroll=4)
 
 
 def translate_kernel(linked, count, *refs):
@@ -269,15 +269,12 @@
 
 
 def descend_kernel(
-    place, scale, tile, octant_far, incoming, interp, cosines, sines, out_far,
-    octant, even, odd, total, out, sent, ready,
+    place, scale, tile, octant, incoming, interp, cosines, sines, out_far,
+    even, odd, total, out, sent,
 ):
     low, high = interp.shape
     count = high // tile
     boxes = even.shape[0] // PAIR
-    octant_copy = pltpu.make_async_copy(octant_far, octant, ready)
-    octant_copy.start()
-    octant_copy.wait()
 
     def shift(i, shifted):
         for lane in range(0, tile, LANES):
@@ -324,20 +321,17 @@
     tile = TILE3
     near = pl.BlockSpec(memory_space=pltpu.VMEM)
     far = pl.BlockSpec(memory_space=pltpu.HBM)
-    octant = pltpu.with_memory_space_constraint(octant, pltpu.HBM)
     return pl.pallas_call(
         functools.partial(descend_kernel, place, low / high, tile),
         out_shape=jax.ShapeDtypeStruct((rows, low), jnp.bfloat16),
-        in_specs=[far, near, near, near, near],
+        in_specs=[pl.BlockSpec(memory_space=pltpu.SMEM), near, near, near, near],
         out_specs=far,
         scratch_shapes=[
-            pltpu.SMEM(octant.shape, octant.dtype),
             pltpu.VMEM((rows, tile), jnp.bfloat16),
             pltpu.VMEM((rows, tile), jnp.bfloat16),
             pltpu.VMEM((low, rows), jnp.float32),
             pltpu.VMEM((rows, low), jnp.bfloat16),
-            pltpu.SemaphoreType.DMA((4,)),
-            pltpu.SemaphoreType.DMA(()),
+            pltpu.SemaphoreType.DMA((8,)),
         ],
         compiler_params=pltpu.CompilerParams(vmem_limit_bytes=12 * MIB),
         cost_estimate=pl.CostEstimate(

time: 44.8 us -> 44.6 us (level)
  no operation moved by 1% of the time
where the time goes in v3:
time: 44.6 us; the launch traced here: 44.4 us
  Pallas kernels  14.1 us (32%)
  blocking collectives  12.6 us (28%)
  starting transfers between devices  9.11 us (20%)
  waiting for transfers between devices  8.13 us (18%)
    all_to_all x1, blocking collectives, local(): lax.all_to_all(incoming, axes, split_axis=0, concat_axis=0, tiled=True)  12.6 us
    all_to_all x1, starting transfers between devices, local(): lax.all_to_all(outgoing, axes, split_axis=0, concat_axis=0, tiled=True)  7.33 us
    pallas_call x1, Pallas kernels, lift(): pl.pallas_call(functools.partial(lift_kernel, place, tile), out_shape=(ja...  6.73 us
    all_to_all x1, waiting for transfers between devices, local(): lax.all_to_all(outgoing, axes, split_axis=0, concat_axis=0, tiled=True)  6.15 us
    pallas_call x1, Pallas kernels, descend(): pl.pallas_call(functools.partial(descend_kernel, place, low / high, tile)...  4.11 us
    pallas_call x1, Pallas kernels, translate(): pl.pallas_call(kernel, out_shape=jax.ShapeDtypeStruct(received.shape, jnp...  3.27 us
    ppermute x1, waiting for transfers between devices, local(): lax.ppermute(code, 'box', [((s + shift) % sides, s) for s in range(sides)])  1.98 us
    ppermute x1, starting transfers between devices, local(): lax.ppermute(code, 'box', [((s + shift) % sides, s) for s in range(sides)])  1.77 us
  transfers between devices with their start and end apart: 2, of which 2 were waited for; matrix products, arithmetic and copies ran while one was open for 1% of the time, Pallas kernels for 0%

profile of v3, /device:TPU:0, one launch (start us, length us, event | category | flops | bytes accessed | tf_op | source)
XLA Modules:
  0.0 44.4 jit_solution(11132129174999429347)
XLA Ops:
  0.0 0.0 copy-start
  0.0 0.0 copy-start.4
  0.0 6.7 %lift.1 = (bf16[32,32,128]{2,1,0:T(8,128)(2,1)}, f32[32,8,128]{2,1,0:T(8,128)}, f32[32,8,128]{2,1,0:T(8,128)}) custom-call(s32[16]{0:T(128)} %octant.1, bf16[256,1024]{1,0:T(8,128)(2,1)} %bitcast.10, bf16[1024,4096]{1,0:T(8,128)(2,1)} %interp.1, f32[8,4096]{1,0:T(8,128)} %angle_far.1), custom_call_target="tpu_custom_call" | custom-call | flops 2147483648 | bytes 8388608 | tf_op jit(solution)/shard_map/lift/pallas_call | solution.py:144
  6.7 7.3 %all-to-all-start = ((bf16[32,32,128]{2,1,0:T(8,128)(2,1)}), bf16[32,32,128]{2,1,0:T(8,128)(2,1)S(1)}, u32[]{:S(2)}, u32[]{:S(2)}) async-start(bf16[32,32,128]{2,1,0:T(8,128)(2,1)} %get-tuple-element.8), calls=%async_computation | async-start | bytes 524288 | tf_op jit(solution)/shard_map/all_to_all | solution.py:363
  14.1 0.0 copy-done.4
  14.1 0.1 add_multiply_fusion.refs_0_
  14.2 1.8 %collective-permute-start = (s32[32,28]{1,0:T(8,128)S(1)}, s32[32,28]{1,0:T(8,128)S(1)}, u32[]{:S(2)}, u32[]{:S(2)}) collective-permute-start(s32[32,28]{1,0:T(8,128)S(1)} %add_multiply_fusion.refs_0_), channel_id=1, source_target_pairs={{16,0},{0,16},{17,1},{1,17},{18,2},{2,18},{19,3},{3,19},{20,4},{4,... | collective-permute-start | bytes 10760 | tf_op jit(solution)/shard_map/ppermute | solution.py:378
  16.0 0.0 copy-done
  16.0 0.1 constant_dynamic-slice_fusion
  16.1 0.1 pad_bitcast_fusion.refs_3_
  16.2 2.0 %collective-permute-done.refs_1_ = s32[32,28]{1,0:T(8,128)S(1)} collective-permute-done((s32[32,28]{1,0:T(8,128)S(1)}, s32[32,28]{1,0:T(8,128)S(1)}, u32[]{:S(2)}, u32[]{:S(2)}) %collective-permute-start) | collective-permute-done | bytes 3616 | tf_op jit(solution)/shard_map/ppermute | solution.py:378
  18.2 6.1 %all-to-all-done = bf16[32,32,128]{2,1,0:T(8,128)(2,1)S(1)} async-done(((bf16[32,32,128]{2,1,0:T(8,128)(2,1)}), bf16[32,32,128]{2,1,0:T(8,128)(2,1)S(1)}, u32[]{:S(2)}, u32[]{:S(2)}) %all-to-all-start) | async-done | bytes 262176 | tf_op jit(solution)/shard_map/all_to_all | solution.py:363
  24.3 0.0 slice-start
  24.3 0.0 slice-start.1
  24.3 0.0 copy-start.1
  24.3 0.0 copy-start.2
  24.3 0.0 copy-start.3
  24.4 3.3 %translate.1 = bf16[64,16,128]{2,1,0:T(8,128)(2,1)S(1)} custom-call(s32[32,28]{1,0:T(8,128)S(1)} %add_multiply_fusion.refs_0_, s32[32,28]{1,0:T(8,128)S(1)} %collective-permute-done.refs_1_, bf16[64,16,128]{2,1,0:T(8,128)(2,1)S(1)} %bitcast.8, f32[2744,128]{1,0:T(8,128)S(1)} %pad_bitcast_fusion.refs_3_), custom_call_target="tpu_custom_call" | custom-call | flops 4294967296 | bytes 4194304 | tf_op jit(solution)/shard_map/translate/pallas_call | solution.py:259
  27.6 12.6 %all_to_all.10.incoming = bf16[32,32,128]{2,1,0:T(8,128)(2,1)S(1)} all-to-all(bf16[32,32,128]{2,1,0:T(8,128)(2,1)S(1)} %bitcast.9), channel_id=1, replica_groups=mesh['box'=2,'dir'=16] {'box','dir'}, dimensions={0} | all-to-all | bytes 524288 | tf_op jit(solution)/shard_map/all_to_all | solution.py:386
  40.2 0.0 slice-done
  40.2 0.0 slice-done.1
  40.2 0.0 copy-done.1
  40.2 0.0 copy-done.2
  40.2 0.0 copy-done.3
  40.3 4.1 %descend.1 = bf16[256,1024]{1,0:T(8,128)(2,1)} custom-call(s32[16]{0:T(128)S(1)} %copy-done.3, bf16[32,32,128]{2,1,0:T(8,128)(2,1)S(1)} %all_to_all.10.incoming, bf16[1024,4096]{1,0:T(8,128)(2,1)S(1)} %bitcast.7, f32[32,8,128]{2,1,0:T(8,128)S(1)} %copy-done.1, f32[32,8,128]{2,1,0:T(8,128)S(1)} %copy-done.2), custom_call_target="tpu_custom_call" | custom-call | flops 2147483648 | bytes 8388608 | tf_op jit(solution)/shard_map/descend/pallas_call | solution.py:324
  (2 shorter events, 0.0 us)
Async XLA Ops:
  0.0 16.0 %copy-start = (f32[343,2,256]{2,1,0:T(2,128)S(1)}, f32[343,2,256]{2,1,0:T(2,128)}, u32[]{:S(2)}) copy-start(f32[343,2,256]{2,1,0:T(2,128)} %param.12) | copy-start | bytes 2107396
  0.0 14.1 %copy-start.4 = (s32[32,27]{1,0:T(8,128)S(1)}, s32[32,27]{1,0:T(8,128)}, u32[]{:S(2)}) copy-start(s32[32,27]{1,0:T(8,128)} %param.11) | copy-start | bytes 10372
  6.7 17.6 %all-to-all-start = ((bf16[32,32,128]{2,1,0:T(8,128)(2,1)}), bf16[32,32,128]{2,1,0:T(8,128)(2,1)S(1)}, u32[]{:S(2)}, u32[]{:S(2)}) async-start(bf16[32,32,128]{2,1,0:T(8,128)(2,1)} %get-tuple-element.8), calls=%async_computation | async-start | bytes 524288 | tf_op jit(solution)/shard_map/all_to_all | solution.py:363
  14.2 4.0 %collective-permute-start = (s32[32,28]{1,0:T(8,128)S(1)}, s32[32,28]{1,0:T(8,128)S(1)}, u32[]{:S(2)}, u32[]{:S(2)}) collective-permute-start(s32[32,28]{1,0:T(8,128)S(1)} %add_multiply_fusion.refs_0_), channel_id=1, source_target_pairs={{16,0},{0,16},{17,1},{1,17},{18,2},{2,18},{19,3},{3,19},{20,4},{4,... | collective-permute-start | bytes 10760 | tf_op jit(solution)/shard_map/ppermute | solution.py:378
  24.3 15.9 %slice-start = ((s8[8388608]{0:T(1024)(128)(4,1)}), s8[4194304]{0:T(1024)(128)(4,1)S(1)}, s32[]{:S(2)}) async-start(s8[8388608]{0:T(1024)(128)(4,1)} %bitcast.6), calls=%async_computation.2 | async-start | bytes 8388608
  24.3 15.9 %slice-start.1 = ((s8[8388608]{0:T(1024)(128)(4,1)}), s8[4194304]{0:T(1024)(128)(4,1)S(1)}, s32[]{:S(2)}) async-start(s8[8388608]{0:T(1024)(128)(4,1)} %bitcast.6), calls=%async_computation.3 | async-start | bytes 8388608
  24.3 15.9 %copy-start.1 = (f32[32,8,128]{2,1,0:T(8,128)S(1)}, f32[32,8,128]{2,1,0:T(8,128)}, u32[]{:S(2)}) copy-start(f32[32,8,128]{2,1,0:T(8,128)} %get-tuple-element.9.cosines) | copy-start | bytes 393220
  24.3 15.9 %copy-start.2 = (f32[32,8,128]{2,1,0:T(8,128)S(1)}, f32[32,8,128]{2,1,0:T(8,128)}, u32[]{:S(2)}) copy-start(f32[32,8,128]{2,1,0:T(8,128)} %get-tuple-element.10.sines) | copy-start | bytes 393220
  24.3 15.9 %copy-start.3 = (s32[16]{0:T(128)S(1)}, s32[16]{0:T(128)}, u32[]{:S(2)}) copy-start(s32[16]{0:T(128)} %octant.1) | copy-start | bytes 196

commit v4 on v3

--- a/solution.py
+++ b/solution.py
@@ -66,7 +66,7 @@
     leaf_copy.start()
     ahead = min(AHEAD, count)
     for i in range(ahead):
-        column_copy(interp_far, interp, arrived, tile, i).start()
+        column_copy(interp_far, interp, arrived, tile, i).start(priority=min(i, 1))
     angle_copy.wait()
     phases(angle, cosines, sines)
     cosines_copy = pltpu.make_async_copy(cosines, cosines_far, ready.at[3])
@@ -86,9 +86,10 @@
     def rise(i, up):
         column_copy(interp_far, interp, arrived, tile, i).wait()
 
-        @pl.when(i + ahead < count)
+        @pl.when(i == 0)
         def _():
-            column_copy(interp_far, interp, arrived, tile, i + ahead).start()
+            for later in range(ahead, count):
+                column_copy(interp_far, interp, arrived, tile, later).start()
 
         up[...] = jnp.dot(
             leaf[...], interp[:, chunk_of(i, tile)], preferred_element_type=jnp.float32

time: 44.6 us -> 44.5 us (level)
  no operation moved by 1% of the time
where the time goes in v4:
time: 44.5 us; the launch traced here: 44.3 us
  Pallas kernels  14 us (31%)
  blocking collectives  12.6 us (28%)
  starting transfers between devices  9.1 us (20%)
  waiting for transfers between devices  8.13 us (18%)
    all_to_all x1, blocking collectives, local(): lax.all_to_all(incoming, axes, split_axis=0, concat_axis=0, tiled=True)  12.6 us
    all_to_all x1, starting transfers between devices, local(): lax.all_to_all(outgoing, axes, split_axis=0, concat_axis=0, tiled=True)  7.33 us
    pallas_call x1, Pallas kernels, lift(): pl.pallas_call(functools.partial(lift_kernel, place, tile), out_shape=(ja...  6.63 us
    all_to_all x1, waiting for transfers between devices, local(): lax.all_to_all(outgoing, axes, split_axis=0, concat_axis=0, tiled=True)  6.15 us
    pallas_call x1, Pallas kernels, descend(): pl.pallas_call(functools.partial(descend_kernel, place, low / high, tile)...  4.1 us
    pallas_call x1, Pallas kernels, translate(): pl.pallas_call(kernel, out_shape=jax.ShapeDtypeStruct(received.shape, jnp...  3.28 us
    ppermute x1, waiting for transfers between devices, local(): lax.ppermute(code, 'box', [((s + shift) % sides, s) for s in range(sides)])  1.98 us
    ppermute x1, starting transfers between devices, local(): lax.ppermute(code, 'box', [((s + shift) % sides, s) for s in range(sides)])  1.77 us
  transfers between devices with their start and end apart: 2, of which 2 were waited for; matrix products, arithmetic and copies ran while one was open for 1% of the time, Pallas kernels for 0%

profile of v4, /device:TPU:0, one launch (start us, length us, event | category | flops | bytes accessed | tf_op | source)
XLA Modules:
  0.0 44.3 jit_solution(3429448678037632)
XLA Ops:
  0.0 0.0 copy-start
  0.0 0.0 copy-start.4
  0.0 6.6 %lift.1 = (bf16[32,32,128]{2,1,0:T(8,128)(2,1)}, f32[32,8,128]{2,1,0:T(8,128)}, f32[32,8,128]{2,1,0:T(8,128)}) custom-call(s32[16]{0:T(128)} %octant.1, bf16[256,1024]{1,0:T(8,128)(2,1)} %bitcast.10, bf16[1024,4096]{1,0:T(8,128)(2,1)} %interp.1, f32[8,4096]{1,0:T(8,128)} %angle_far.1), custom_call_target="tpu_custom_call" | custom-call | flops 2147483648 | bytes 8388608 | tf_op jit(solution)/shard_map/lift/pallas_call | solution.py:145
  6.6 7.3 %all-to-all-start = ((bf16[32,32,128]{2,1,0:T(8,128)(2,1)}), bf16[32,32,128]{2,1,0:T(8,128)(2,1)S(1)}, u32[]{:S(2)}, u32[]{:S(2)}) async-start(bf16[32,32,128]{2,1,0:T(8,128)(2,1)} %get-tuple-element.8), calls=%async_computation | async-start | bytes 524288 | tf_op jit(solution)/shard_map/all_to_all | solution.py:364
  14.0 0.0 copy-done.4
  14.0 0.1 add_multiply_fusion.refs_0_
  14.1 1.8 %collective-permute-start = (s32[32,28]{1,0:T(8,128)S(1)}, s32[32,28]{1,0:T(8,128)S(1)}, u32[]{:S(2)}, u32[]{:S(2)}) collective-permute-start(s32[32,28]{1,0:T(8,128)S(1)} %add_multiply_fusion.refs_0_), channel_id=1, source_target_pairs={{16,0},{0,16},{17,1},{1,17},{18,2},{2,18},{19,3},{3,19},{20,4},{4,... | collective-permute-start | bytes 10760 | tf_op jit(solution)/shard_map/ppermute | solution.py:379
  15.9 0.0 copy-done
  15.9 0.1 constant_dynamic-slice_fusion
  16.0 0.1 pad_bitcast_fusion.refs_3_
  16.1 2.0 %collective-permute-done.refs_1_ = s32[32,28]{1,0:T(8,128)S(1)} collective-permute-done((s32[32,28]{1,0:T(8,128)S(1)}, s32[32,28]{1,0:T(8,128)S(1)}, u32[]{:S(2)}, u32[]{:S(2)}) %collective-permute-start) | collective-permute-done | bytes 3616 | tf_op jit(solution)/shard_map/ppermute | solution.py:379
  18.1 6.1 %all-to-all-done = bf16[32,32,128]{2,1,0:T(8,128)(2,1)S(1)} async-done(((bf16[32,32,128]{2,1,0:T(8,128)(2,1)}), bf16[32,32,128]{2,1,0:T(8,128)(2,1)S(1)}, u32[]{:S(2)}, u32[]{:S(2)}) %all-to-all-start) | async-done | bytes 262176 | tf_op jit(solution)/shard_map/all_to_all | solution.py:364
  24.2 0.0 slice-start
  24.2 0.0 slice-start.1
  24.2 0.0 copy-start.1
  24.2 0.0 copy-start.2
  24.2 0.0 copy-start.3
  24.3 3.3 %translate.1 = bf16[64,16,128]{2,1,0:T(8,128)(2,1)S(1)} custom-call(s32[32,28]{1,0:T(8,128)S(1)} %add_multiply_fusion.refs_0_, s32[32,28]{1,0:T(8,128)S(1)} %collective-permute-done.refs_1_, bf16[64,16,128]{2,1,0:T(8,128)(2,1)S(1)} %bitcast.8, f32[2744,128]{1,0:T(8,128)S(1)} %pad_bitcast_fusion.refs_3_), custom_call_target="tpu_custom_call" | custom-call | flops 4294967296 | bytes 4194304 | tf_op jit(solution)/shard_map/translate/pallas_call | solution.py:260
  27.5 12.6 %all_to_all.10.incoming = bf16[32,32,128]{2,1,0:T(8,128)(2,1)S(1)} all-to-all(bf16[32,32,128]{2,1,0:T(8,128)(2,1)S(1)} %bitcast.9), channel_id=1, replica_groups=mesh['box'=2,'dir'=16] {'box','dir'}, dimensions={0} | all-to-all | bytes 524288 | tf_op jit(solution)/shard_map/all_to_all | solution.py:387
  40.1 0.0 slice-done
  40.1 0.0 slice-done.1
  40.1 0.0 copy-done.1
  40.1 0.0 copy-done.2
  40.2 0.0 copy-done.3
  40.2 4.1 %descend.1 = bf16[256,1024]{1,0:T(8,128)(2,1)} custom-call(s32[16]{0:T(128)S(1)} %copy-done.3, bf16[32,32,128]{2,1,0:T(8,128)(2,1)S(1)} %all_to_all.10.incoming, bf16[1024,4096]{1,0:T(8,128)(2,1)S(1)} %bitcast.7, f32[32,8,128]{2,1,0:T(8,128)S(1)} %copy-done.1, f32[32,8,128]{2,1,0:T(8,128)S(1)} %copy-done.2), custom_call_target="tpu_custom_call" | custom-call | flops 2147483648 | bytes 8388608 | tf_op jit(solution)/shard_map/descend/pallas_call | solution.py:325
  (2 shorter events, 0.0 us)
Async XLA Ops:
  0.0 15.9 %copy-start = (f32[343,2,256]{2,1,0:T(2,128)S(1)}, f32[343,2,256]{2,1,0:T(2,128)}, u32[]{:S(2)}) copy-start(f32[343,2,256]{2,1,0:T(2,128)} %param.12) | copy-start | bytes 2107396
  0.0 14.0 %copy-start.4 = (s32[32,27]{1,0:T(8,128)S(1)}, s32[32,27]{1,0:T(8,128)}, u32[]{:S(2)}) copy-start(s32[32,27]{1,0:T(8,128)} %param.11) | copy-start | bytes 10372
  6.6 17.6 %all-to-all-start = ((bf16[32,32,128]{2,1,0:T(8,128)(2,1)}), bf16[32,32,128]{2,1,0:T(8,128)(2,1)S(1)}, u32[]{:S(2)}, u32[]{:S(2)}) async-start(bf16[32,32,128]{2,1,0:T(8,128)(2,1)} %get-tuple-element.8), calls=%async_computation | async-start | bytes 524288 | tf_op jit(solution)/shard_map/all_to_all | solution.py:364
  14.1 4.0 %collective-permute-start = (s32[32,28]{1,0:T(8,128)S(1)}, s32[32,28]{1,0:T(8,128)S(1)}, u32[]{:S(2)}, u32[]{:S(2)}) collective-permute-start(s32[32,28]{1,0:T(8,128)S(1)} %add_multiply_fusion.refs_0_), channel_id=1, source_target_pairs={{16,0},{0,16},{17,1},{1,17},{18,2},{2,18},{19,3},{3,19},{20,4},{4,... | collective-permute-start | bytes 10760 | tf_op jit(solution)/shard_map/ppermute | solution.py:379
  24.2 15.9 %slice-start = ((s8[8388608]{0:T(1024)(128)(4,1)}), s8[4194304]{0:T(1024)(128)(4,1)S(1)}, s32[]{:S(2)}) async-start(s8[8388608]{0:T(1024)(128)(4,1)} %bitcast.6), calls=%async_computation.2 | async-start | bytes 8388608
  24.2 15.9 %slice-start.1 = ((s8[8388608]{0:T(1024)(128)(4,1)}), s8[4194304]{0:T(1024)(128)(4,1)S(1)}, s32[]{:S(2)}) async-start(s8[8388608]{0:T(1024)(128)(4,1)} %bitcast.6), calls=%async_computation.3 | async-start | bytes 8388608
  24.2 15.9 %copy-start.1 = (f32[32,8,128]{2,1,0:T(8,128)S(1)}, f32[32,8,128]{2,1,0:T(8,128)}, u32[]{:S(2)}) copy-start(f32[32,8,128]{2,1,0:T(8,128)} %get-tuple-element.9.cosines) | copy-start | bytes 393220
  24.2 15.9 %copy-start.2 = (f32[32,8,128]{2,1,0:T(8,128)S(1)}, f32[32,8,128]{2,1,0:T(8,128)}, u32[]{:S(2)}) copy-start(f32[32,8,128]{2,1,0:T(8,128)} %get-tuple-element.10.sines) | copy-start | bytes 393220
  24.2 15.9 %copy-start.3 = (s32[16]{0:T(128)S(1)}, s32[16]{0:T(128)}, u32[]{:S(2)}) copy-start(s32[16]{0:T(128)} %octant.1) | copy-start | bytes 196
